TPU v7x, 256 devices: a whole 4x4x8 slice. The times are simulated.
256 devices in a mesh: pulse: 8 (over y_lo, x), tile: 32 (over z, y_hi, core).
Axes of the slice: x: 4, y: 4 (y_hi: 2, y_lo: 2; y = y_hi * 2 + y_lo), z: 8, core: 2. Of those that a mesh axis runs over, the one named last changes fastest.
Arguments:
- pulses: bfloat16 [4096, 2, 32768], P(None, None, ('pulse', 'tile')), may hold values from -6 to 6
- steering: bfloat16 [2, 128, 128], replicated, may hold values from -0.375 to 0.375
- merge_re: bfloat16 [3, 256, 256], replicated, may hold values from -0.25 to 0.25
- merge_im: bfloat16 [3, 256, 256], replicated, may hold values from -0.25 to 0.25
- range_shift: int32 [3, 2, 128], replicated, may hold values from -8 to 8
- image_map: bfloat16 [8, 32, 2, 128, 512], P('pulse', 'tile'), may hold values from -0.0234375 to 0.0234375
Outputs:
- image: float32 [4096, 1024], P(('pulse', 'tile'))
All inputs are finite; a program needn't handle non-finite values.
Results may differ from a plain program's by a relative error of at most 0.0057.
Values may be sent and summed in bfloat16 or wider, within the bound.
No kernel may reach another device: no remote copies, remote signals or barrier semaphores. Data moves between devices by JAX's collectives and lax.ppermute only.
A program may use at most 64 MiB of HBM per device.

v0:
```python
import functools

import jax
import jax.numpy as jnp
from jax import lax
from jax.experimental import pallas as pl
from jax.experimental.pallas import tpu as pltpu
from jax.sharding import PartitionSpec as P


SHIFT = 8
SET = 8
VMEM = pl.BlockSpec(memory_space=pltpu.VMEM)
SMEM = pl.BlockSpec(memory_space=pltpu.SMEM)


def swapped(index):
    return ((index >> 1) & 1) << 2 | ((index >> 2) & 1) << 1 | (index & 1)


def weights_kernel(member_ref, steering_ref, merge_re_ref, merge_im_ref, steer_ref, merge_ref):
    def block(out, real, imag):
        high, wide = real.shape
        out[:high, :wide] = real
        out[:high, wide:] = imag
        out[high:, :wide] = -imag
        out[high:, wide:] = real

    def arranged(matrix, bit):
        count = matrix.shape[0] // 2
        turned = jnp.concatenate([matrix[count:], matrix[:count]], axis=0)
        turned = jnp.concatenate([turned[:, count:], turned[:, :count]], axis=1)
        return jnp.where(bit == 1, turned, matrix)

    block(steer_ref, steering_ref[0], steering_ref[1])
    for level in range(merge_re_ref.shape[0]):
        bit = (member_ref[0] >> level) & 1
        block(
            merge_ref.at[level], arranged(merge_re_ref[level], bit), arranged(merge_im_ref[level], bit)
        )


def windows_kernel(own, halo, member_ref, raw_ref, *rest):
    outs, sems = rest[: SET + 2], rest[SET + 2]
    member = member_ref[0]
    main, edge = 2 * own, 2 * halo
    early = own + edge

    def each(action):
        for slot in range(SET):
            block = swapped(member ^ slot)
            start = block * main

            def move(kind, source, out, target, length):
                made = pltpu.make_async_copy(
                    raw_ref.at[pl.ds(pl.multiple_of(source, 16), length), :],
                    out.at[pl.ds(target, length), :],
                    sems.at[slot, kind],
                )
                action(made)

            out = outs[slot]
            if slot < SET - 2:
                last, place = out, edge + main
                move(0, start, out, edge, main)
            else:
                last, place = outs[slot + 2], main - early
                move(0, start, out, edge, early)
                move(3, start + early, last, 0, main - early)

            @pl.when(block > 0)
            def _():
                move(1, start - edge, out, 0, edge)

            @pl.when(block < SET - 1)
            def _():
                move(2, start + main, last, place, edge)

    each(lambda made: made.start())
    zeros = jnp.zeros((edge, raw_ref.shape[1]), raw_ref.dtype)
    for slot in range(SET):
        block = swapped(member ^ slot)
        last = outs[slot] if slot < SET - 2 else outs[slot + 2]

        @pl.when(block == 0)
        def _():
            outs[slot][:edge, :] = zeros

        @pl.when(block == SET - 1)
        def _():
            last[last.shape[0] - edge :, :] = zeros

    each(lambda made: made.wait())


def moved_rows(value, table):
    pick, before, after = table
    chunk = value.shape[0] - 2 * SHIFT
    value = value.astype(jnp.float32)
    turned = [
        jnp.take_along_axis(value[tile * SHIFT : (tile + 1) * SHIFT], pick, axis=0)
        for tile in range(chunk // SHIFT + 2)
    ]
    moved = [
        jnp.where(before, turned[tile], jnp.where(after, turned[tile + 2], turned[tile + 1]))
        for tile in range(chunk // SHIFT)
    ]
    return jnp.concatenate(moved, axis=0).astype(jnp.bfloat16)


def merge_level(rows, level, pairs, member, load, sources, merge, shift_ref, emit):
    count = shift_ref.shape[2]
    sublane = lax.broadcasted_iota(jnp.int32, (SHIFT, count), 0)
    bit = (member >> level) & 1
    lower, upper = shift_ref[level, 0:1, :], shift_ref[level, 1:2, :]
    tables = []
    for own, other in ((lower, upper), (upper, lower)):
        offset = jnp.broadcast_to(jnp.where(bit == 0, own, other), (SHIFT, count)) + sublane
        tables.append((offset & (SHIFT - 1), offset < 0, offset >= SHIFT))

    def fill(at):
        target = sources[at % 2]
        for side in range(2):
            for part in range(2):
                column = (2 * part + side) * count
                low = 0
                while low < rows:
                    chunk = min(112, rows - low)
                    value = load(pairs[at][side], part, slice(low, low + chunk + 2 * SHIFT))
                    target[low : low + chunk, column : column + count] = moved_rows(value, tables[side])
                    low += chunk

    fill(0)
    for at, ends in enumerate(pairs):
        if at + 1 < len(pairs):
            fill(at + 1)
        for part in range(2):
            result = jnp.dot(
                sources[at % 2][...],
                merge[:, 2 * part * count : 2 * (part + 1) * count],
                preferred_element_type=jnp.float32,
            ).astype(jnp.bfloat16)
            for side in range(2):
                emit(ends[side], part, result[:, side * count : (side + 1) * count])


def fill_guards(beams, slots, rows):
    zeros = jnp.zeros((SHIFT, beams.shape[-1]), beams.dtype)
    for slot in range(slots):
        for part in range(2):
            beams[slot, part, :SHIFT, :] = zeros
            beams[slot, part, SHIFT + rows :, :] = zeros


def clear_outside(halo, member, beams, slots, ends):
    zeros = jnp.zeros((halo, beams.shape[-1]), beams.dtype)
    for end in ends:
        at = SHIFT if end == 0 else beams.shape[2] - SHIFT - halo

        @pl.when(member == end)
        def _():
            for slot in range(slots):
                for part in range(2):
                    beams[slot, part, at : at + halo, :] = zeros


def start_kernel(rows, halo, known, ends, member_ref, *rest):
    many = 2 if known else 1
    sources_of, rest = (rest[:many], rest[many : 2 * many]), rest[2 * many :]
    steer_ref, merge_ref, shift_ref, out_ref, beams, *sources, spread = rest
    count = steer_ref.shape[1] // 2
    member = member_ref[0]
    fill_guards(beams, 2, rows)
    fill_guards(out_ref, 2, rows)
    for slot, raw_refs in enumerate(sources_of):
        if known:
            spread[:known, :] = raw_refs[0][raw_refs[0].shape[0] - known :, :].astype(jnp.float32)
        spread[known:, :] = raw_refs[-1][...].astype(jnp.float32)
        real = spread[pl.ds(0, rows, stride=2), :].astype(jnp.bfloat16)
        imag = spread[pl.ds(1, rows, stride=2), :].astype(jnp.bfloat16)
        result = jnp.dot(
            jnp.concatenate([real, imag], axis=1), steer_ref[...], preferred_element_type=jnp.float32
        ).astype(jnp.bfloat16)
        beams[slot, 0, pl.ds(SHIFT, rows), :] = result[:, :count]
        beams[slot, 1, pl.ds(SHIFT, rows), :] = result[:, count:]

    def emit(slot, part, value):
        out_ref[slot, part, pl.ds(SHIFT, rows), :] = value

    def load(slot, part, window):
        return beams[slot, part, window, :]

    merge_level(rows, 0, [(0, 1)], member, load, sources, merge_ref.at[0], shift_ref, emit)
    clear_outside(halo, member, out_ref, 2, ends)


def middle_kernel(rows, halo, member_ref, left_ref, right_ref, merge_ref, shift_ref, out_ref, *sources):
    member = member_ref[0]
    fill_guards(out_ref, SET // 2, rows)

    def load(slot, part, window):
        return (left_ref, right_ref)[slot // 2][slot % 2, part, window, :]

    def emit(slot, part, value):
        out_ref[slot, part, pl.ds(SHIFT, rows), :] = value

    merge_level(rows, 1, [(0, 2), (1, 3)], member, load, sources, merge_ref.at[1], shift_ref, emit)
    clear_outside(halo, member, out_ref, SET // 2, (0, SET - 1))


def finish_kernel(
    rows, halo, begin, end, member_ref, middle_ref, left_ref, right_ref, merge_ref, shift_ref, out_ref,
    high, *sources,
):
    member = member_ref[0]
    fill_guards(high, SET // 2, rows)

    def within(window):
        return slice(begin + window.start, begin + window.stop)

    def load_pairs(slot, part, window):
        if slot < 2:
            return left_ref[slot, part, within(window), :]
        return right_ref[slot - 2, part, window, :]

    def load_all(slot, part, window):
        if slot < SET // 2:
            return middle_ref[slot, part, within(window), :]
        return high[slot - SET // 2, part, window, :]

    def keep(slot, part, value):
        high[slot, part, pl.ds(SHIFT, rows), :] = value

    def last(slot, part, value):
        out_ref[slot, part] = value[halo : rows - halo]

    merge_level(
        rows, 1, [(0, 2), (1, 3)], member, load_pairs, sources, merge_ref.at[1], shift_ref, keep
    )
    clear_outside(halo, member, high, SET // 2, (end,))
    pairs = [(slot, slot + SET // 2) for slot in range(SET // 2)]
    merge_level(rows, 2, pairs, member, load_all, sources, merge_ref.at[2], shift_ref, last)


def image_kernel(groups, *rest):
    known_refs, (beams_ref, *rest) = rest[: len(rest) - SET - 4], rest[len(rest) - SET - 4 :]
    maps, halves, out_ref = rest[: SET - 2], rest[SET - 2 : SET + 2], rest[SET + 2]
    own = beams_ref.shape[2]
    width = maps[0].shape[1]
    piece = out_ref.shape[2]
    first = 0
    if known_refs:
        first = known_refs[0].shape[1]
        out_ref[:, :first] = known_refs[0][...]
    values = [ref[...] for ref in maps] + [
        jnp.concatenate([halves[at][...], halves[at + 1][...]], axis=0) for at in (0, 2)
    ]
    for half in range(2):
        total = jnp.zeros((own, width), jnp.float32)
        for slot in range(SET):
            real, imag = beams_ref[slot, 0], beams_ref[slot, 1]
            left = jnp.concatenate([real, -imag] if half == 0 else [imag, real], axis=1)
            total += jnp.dot(left, values[slot], preferred_element_type=jnp.float32)
        total = total.astype(jnp.bfloat16)
        for at in range(own // piece):
            out_ref[
                swapped(at % groups), first + at // groups, :, half * width : (half + 1) * width
            ] = total[at * piece : (at + 1) * piece]


def sum_kernel(pieces_ref, out_ref):
    total = pieces_ref[0].astype(jnp.float32)
    for source in range(1, pieces_ref.shape[0]):
        total += pieces_ref[source].astype(jnp.float32)
    total = total.astype(jnp.bfloat16)
    out_ref[0] = total
    out_ref[1] = total


def last_kernel(half_ref, pieces_ref, out_ref):
    many = pieces_ref.shape[0] // 2
    base = half_ref[0] * many
    total = pieces_ref[base].astype(jnp.float32)
    for source in range(1, many):
        total += pieces_ref[base + source].astype(jnp.float32)
    out_ref[...] = total


def call(kernel, out_shape, in_specs, scratch=(), flops=0, vmem=24, out_specs=None):
    def run(*operands):
        return called(kernel, out_shape, in_specs, scratch, flops, vmem, out_specs)(*operands)

    return run


def called(kernel, out_shape, in_specs, scratch, flops, vmem, out_specs):
    return pl.pallas_call(
        kernel,
        out_shape=out_shape,
        in_specs=in_specs,
        out_specs=jax.tree.map(lambda _: VMEM, out_shape) if out_specs is None else out_specs,
        scratch_shapes=scratch,
        cost_estimate=pl.CostEstimate(flops=flops, bytes_accessed=2**20, transcendentals=0),
        compiler_params=pltpu.CompilerParams(vmem_limit_bytes=vmem * 2**20),
    )


def body(pulses, steering, merge_re, merge_im, range_shift, image_map):
    total_rows = pulses.shape[0]
    count = steering.shape[2]
    levels = merge_re.shape[0]
    groups = lax.axis_size("pulse")
    tiles = lax.axis_size("tile")
    sets = tiles // SET
    own = total_rows // SET
    halo = levels * SHIFT
    rows = own + 2 * halo
    piece = own // tiles
    half_type = jnp.bfloat16
    member = lax.axis_index("tile") % SET
    where = member.reshape(1).astype(jnp.int32)

    def swap(value, mask):
        return lax.ppermute(value, "tile", [(s, s ^ mask) for s in range(tiles)])

    part = own // 2 + 2 * halo
    raw = pulses.reshape(2 * total_rows, count)
    lengths = [2 * rows] * (SET - 2) + [2 * part] * 2 + [own] * 2
    windows = call(
        functools.partial(windows_kernel, own, halo),
        [jax.ShapeDtypeStruct((length, count), half_type) for length in lengths],
        [SMEM, pl.BlockSpec(memory_space=pltpu.HBM)],
        scratch=[pltpu.SemaphoreType.DMA((SET, 4))],
    )(where, raw)
    arrived = {0: windows[0]}
    for mask in range(1, SET):
        arrived[mask] = swap(windows[mask], mask)
    late = [swap(windows[mask + 2], mask) for mask in (6, 7)]

    own_map = image_map.reshape(2 * count, -1)
    width = own_map.shape[1]
    held = {0: own_map}
    for mask in (2, 4):
        held[mask] = swap(own_map, mask)
    for slot in (0, 2, 4):
        held[slot | 1] = swap(held[slot], 1)
    far = (swap(held[4][:count], 2), swap(held[2][count:], 4))
    near = (swap(far[0], 1), swap(far[1], 1))

    steer_block, merge_block = call(
        weights_kernel,
        [
            jax.ShapeDtypeStruct((2 * count, 2 * count), half_type),
            jax.ShapeDtypeStruct((levels, 4 * count, 4 * count), half_type),
        ],
        [SMEM] + [VMEM] * 3,
        flops=10**8,
    )(where, steering, merge_re, merge_im)

    def start(length, known, ends, *windows):
        return call(
            functools.partial(start_kernel, length, halo, known, ends),
            jax.ShapeDtypeStruct((2, 2, length + 2 * SHIFT, count), half_type),
            [SMEM] + [VMEM] * (3 + len(windows)),
            scratch=[
                pltpu.VMEM((2, 2, length + 2 * SHIFT, count), half_type),
                pltpu.VMEM((length, 4 * count), half_type),
                pltpu.VMEM((2 * length, count), jnp.float32),
            ],
            flops=5 * 10**8,
        )(where, *windows, steer_block, merge_block, range_shift)

    started = [
        start(rows, 0, (0, SET - 1), arrived[base], arrived[base + 1])
        for base in range(0, SET - 2, 2)
    ]
    middle = call(
        functools.partial(middle_kernel, rows, halo),
        jax.ShapeDtypeStruct((SET // 2, 2, rows + 2 * SHIFT, count), half_type),
        [SMEM] + [VMEM] * 4,
        scratch=[pltpu.VMEM((rows, 4 * count), half_type)] * 2,
        flops=6 * 10**8,
    )(where, started[0], started[1], merge_block, range_shift)
    partial_rows = ()
    for step in range(2):
        if step == 0:
            ending = start(part, 0, (0,), arrived[6], arrived[7])
        else:
            ending = start(part, 4 * halo, (SET - 1,), arrived[6], late[0], arrived[7], late[1])
        beams = call(
            functools.partial(finish_kernel, part, halo, step * own // 2, step * (SET - 1)),
            jax.ShapeDtypeStruct((SET, 2, own // 2, count), half_type),
            [SMEM] + [VMEM] * 5,
            scratch=[pltpu.VMEM((SET // 2, 2, part + 2 * SHIFT, count), half_type)]
            + [pltpu.VMEM((part, 4 * count), half_type)] * 2,
            flops=10**9,
        )(where, middle, started[2], ending, merge_block, range_shift)
        partial_rows = (
            call(
                functools.partial(image_kernel, groups),
                jax.ShapeDtypeStruct((groups, (1 + step) * sets // 2, piece, 2 * width), half_type),
                [VMEM] * (3 + SET + step),
                flops=10**9,
            )(*partial_rows, beams, *[held[slot] for slot in range(SET - 2)], *far, *near),
        )
    partial_rows = partial_rows[0]

    pieces = lax.all_to_all(partial_rows, "pulse", 0, 0, tiled=True)
    doubled = call(
        sum_kernel, jax.ShapeDtypeStruct((2, sets, piece, 2 * width), half_type), [VMEM]
    )(pieces)

    def device(pulse, u, i):
        return pulse * tiles + u * SET + swapped(i)

    crossing = []
    for a in range(groups):
        for b in range(a + 1, groups):
            crossing.append(
                [device(a, u, b) for u in range(sets)] + [device(b, u, a) for u in range(sets)]
            )
    for a in range(0, groups, 2):
        crossing.append(
            [device(a, u, a) for u in range(sets)] + [device(a + 1, u, a + 1) for u in range(sets)]
        )
    last = lax.all_to_all(
        doubled.reshape(2 * sets, piece, 2 * width),
        ("pulse", "tile"),
        0,
        0,
        axis_index_groups=crossing,
        tiled=True,
    )
    pulse = lax.axis_index("pulse")
    target = swapped(member)
    half = jnp.where(pulse == target, pulse % 2, (pulse < target).astype(jnp.int32))
    return call(
        last_kernel, jax.ShapeDtypeStruct((piece, 2 * width), jnp.float32), [SMEM, VMEM]
    )(half.reshape(1).astype(jnp.int32), last)


def solution(mesh):
    placed = (
        P(None, None, ("pulse", "tile")),
        P(),
        P(),
        P(),
        P(),
        P("pulse", "tile", None, None, None),
    )
    return jax.shard_map(
        body, mesh=mesh, in_specs=placed, out_specs=P(("pulse", "tile"), None), check_vma=False
    )
```

profile of v0, /device:TPU:48, one launch (start us, length us, event | category | flops | bytes accessed | tf_op | source)
XLA Modules:
  0.0 96.8 jit_solution(17660401024597924524)
XLA Ops:
  0.0 1.6 %copy-done = bf16[4096,2,128]{2,1,0:T(2,128)(2,1)S(1)} copy-done((bf16[4096,2,128]{2,1,0:T(2,128)(2,1)S(1)}, bf16[4096,2,128]{2,1,0:T(2,128)(2,1)}, u32[]{:S(2)}) %copy-start) | copy-done | bytes 2097176
  1.6 1.5 %shard_map.64 = (bf16[1120,128]{1,0:T(8,128)(2,1)S(1)}, bf16[1120,128]{1,0:T(8,128)(2,1)S(1)}, bf16[1120,128]{1,0:T(8,128)(2,1)S(1)}, bf16[1120,128]{1,0:T(8,128...) custom-call(s32[1]{0:T(128)} %bitcast.1.member_ref, ...), custom_call_target="tpu_custom_call" | custom-call | bytes 1048576 | tf_op jit(solution)/shard_map/pallas_call | solution.py:291
  3.1 1.7 %collective-permute-start.16 = (bf16[512,128]{1,0:T(8,128)(2,1)S(1)}, bf16[512,128]{1,0:T(8,128)(2,1)S(1)}, u32[]{:S(2)}, u32[]{:S(2)}) collective-permute-start(bf16[512,128]{1,0:T(8,128)(2,1)S(1)} %get-tuple-element.27), channel_id=1, source_target_pairs={{0,6},{1,7},{2,4},{3,5},{4,2},{5,3},{6,0},{7,1},{8,14},{9,15},{10,... | collective-permute-start | bytes 393224 | tf_op jit(solution)/shard_map/ppermute | solution.py:324
  5.0 3.2 %collective-permute-start.8 = (bf16[256,512]{1,0:T(8,128)(2,1)S(1)}, bf16[256,512]{1,0:T(8,128)(2,1)S(1)}, u32[]{:S(2)}, u32[]{:S(2)}) collective-permute-start(bf16[256,512]{1,0:T(8,128)(2,1)S(1)} %bitcast.7), channel_id=1, source_target_pairs={{0,2},{1,3},{2,0},{3,1},{4,6},{5,7},{6,4},{7,5},{8,10},{9,11},{10,... | collective-permute-start | bytes 786440 | tf_op jit(solution)/shard_map/ppermute | solution.py:324
  8.2 1.6 %collective-permute-start.5 = (bf16[608,128]{1,0:T(8,128)(2,1)S(1)}, bf16[608,128]{1,0:T(8,128)(2,1)S(1)}, u32[]{:S(2)}, u32[]{:S(2)}) collective-permute-start(bf16[608,128]{1,0:T(8,128)(2,1)S(1)} %get-tuple-element.25), channel_id=1, source_target_pairs={{0,6},{1,7},{2,4},{3,5},{4,2},{5,3},{6,0},{7,1},{8,14},{9,15},{10,... | collective-permute-start | bytes 466952 | tf_op jit(solution)/shard_map/ppermute | solution.py:324
  9.8 1.2 %collective-permute-start.17 = (bf16[512,128]{1,0:T(8,128)(2,1)S(1)}, bf16[512,128]{1,0:T(8,128)(2,1)S(1)}, u32[]{:S(2)}, u32[]{:S(2)}) collective-permute-start(bf16[512,128]{1,0:T(8,128)(2,1)S(1)} %get-tuple-element.28), channel_id=1, source_target_pairs={{0,7},{1,6},{2,5},{3,4},{4,3},{5,2},{6,1},{7,0},{8,15},{9,14},{10,... | collective-permute-start | bytes 393224 | tf_op jit(solution)/shard_map/ppermute | solution.py:324
  11.0 1.0 %collective-permute-done.16.rest_1_ = bf16[512,128]{1,0:T(8,128)(2,1)S(1)} collective-permute-done((bf16[512,128]{1,0:T(8,128)(2,1)S(1)}, bf16[512,128]{1,0:T(8,128)(2,1)S(1)}, u32[]{:S(2)}, u32[]{:S(2)}) %collective-permute-start.16) | collective-permute-done | bytes 131104 | tf_op jit(solution)/shard_map/ppermute | solution.py:324
  12.0 2.0 %collective-permute-start.6 = (bf16[608,128]{1,0:T(8,128)(2,1)S(1)}, bf16[608,128]{1,0:T(8,128)(2,1)S(1)}, u32[]{:S(2)}, u32[]{:S(2)}) collective-permute-start(bf16[608,128]{1,0:T(8,128)(2,1)S(1)} %get-tuple-element.26), channel_id=1, source_target_pairs={{0,7},{1,6},{2,5},{3,4},{4,3},{5,2},{6,1},{7,0},{8,15},{9,14},{10,... | collective-permute-start | bytes 466952 | tf_op jit(solution)/shard_map/ppermute | solution.py:324
  14.0 7.5 %collective-permute-done.17.rest_3_ = bf16[512,128]{1,0:T(8,128)(2,1)S(1)} collective-permute-done((bf16[512,128]{1,0:T(8,128)(2,1)S(1)}, bf16[512,128]{1,0:T(8,128)(2,1)S(1)}, u32[]{:S(2)}, u32[]{:S(2)}) %collective-permute-start.17) | collective-permute-done | bytes 131104 | tf_op jit(solution)/shard_map/ppermute | solution.py:324
  21.6 3.6 %collective-permute-start.4 = (bf16[1120,128]{1,0:T(8,128)(2,1)S(1)}, bf16[1120,128]{1,0:T(8,128)(2,1)S(1)}, u32[]{:S(2)}, u32[]{:S(2)}) collective-permute-start(bf16[1120,128]{1,0:T(8,128)(2,1)S(1)} %get-tuple-element.24), channel_id=1, source_target_pairs={{0,5},{1,4},{2,7},{3,6},{4,1},{5,0},{6,3},{7,2},{8,13},{9,12},{10,... | collective-permute-start | bytes 860168 | tf_op jit(solution)/shard_map/ppermute | solution.py:324
  25.6 3.0 %collective-permute-start.2 = (bf16[1120,128]{1,0:T(8,128)(2,1)S(1)}, bf16[1120,128]{1,0:T(8,128)(2,1)S(1)}, u32[]{:S(2)}, u32[]{:S(2)}) collective-permute-start(bf16[1120,128]{1,0:T(8,128)(2,1)S(1)} %get-tuple-element.22), channel_id=1, source_target_pairs={{0,3},{1,2},{2,1},{3,0},{4,7},{5,6},{6,5},{7,4},{8,11},{9,10},{10,... | collective-permute-start | bytes 860168 | tf_op jit(solution)/shard_map/ppermute | solution.py:324
  29.0 0.5 shard_map.70.right_ref
  29.6 0.5 shard_map.73.right_ref
  30.1 2.6 %collective-permute-start.7 = (bf16[256,512]{1,0:T(8,128)(2,1)S(1)}, bf16[256,512]{1,0:T(8,128)(2,1)S(1)}, u32[]{:S(2)}, u32[]{:S(2)}) collective-permute-start(bf16[256,512]{1,0:T(8,128)(2,1)S(1)} %bitcast.8), channel_id=1, source_target_pairs={{0,1},{1,0},{2,3},{3,2},{4,5},{5,4},{6,7},{7,6},{8,9},{9,8},{10,11... | collective-permute-start | bytes 786440 | tf_op jit(solution)/shard_map/ppermute | solution.py:324
  32.7 4.6 %collective-permute-done.4.rest_1_ = bf16[1120,128]{1,0:T(8,128)(2,1)S(1)} collective-permute-done((bf16[1120,128]{1,0:T(8,128)(2,1)S(1)}, bf16[1120,128]{1,0:T(8,128)(2,1)S(1)}, u32[]{:S(2)}, u32[]{:S(2)}) %collective-permute-start.4) | collective-permute-done | bytes 286752 | tf_op jit(solution)/shard_map/ppermute | solution.py:324
  37.3 1.5 %collective-permute-start.12 = (bf16[128,512]{1,0:T(8,128)(2,1)S(1)}, bf16[128,512]{1,0:T(8,128)(2,1)S(1)}, u32[]{:S(2)}, u32[]{:S(2)}) collective-permute-start(bf16[128,512]{1,0:T(8,128)(2,1)S(1)} %slice.8), channel_id=1, source_target_pairs={{0,2},{1,3},{2,0},{3,1},{4,6},{5,7},{6,4},{7,5},{8,10},{9,11},{10,... | collective-permute-start | bytes 393224 | tf_op jit(solution)/shard_map/ppermute | solution.py:324
  38.8 0.7 shard_map.69.left_ref
  39.5 1.0 %collective-permute-start.13 = (bf16[128,512]{1,0:T(8,128)(2,1)S(1)}, bf16[128,512]{1,0:T(8,128)(2,1)S(1)}, u32[]{:S(2)}, u32[]{:S(2)}) collective-permute-start(bf16[128,512]{1,0:T(8,128)(2,1)S(1)} %slice.9), channel_id=1, source_target_pairs={{0,4},{1,5},{2,6},{3,7},{4,0},{5,1},{6,2},{7,3},{8,12},{9,13},{10,... | collective-permute-start | bytes 393224 | tf_op jit(solution)/shard_map/ppermute | solution.py:324
  40.5 1.2 %collective-permute-done.2.rest_1_ = bf16[1120,128]{1,0:T(8,128)(2,1)S(1)} collective-permute-done((bf16[1120,128]{1,0:T(8,128)(2,1)S(1)}, bf16[1120,128]{1,0:T(8,128)(2,1)S(1)}, u32[]{:S(2)}, u32[]{:S(2)}) %collective-permute-start.2) | collective-permute-done | bytes 286752 | tf_op jit(solution)/shard_map/ppermute | solution.py:324
  41.8 0.7 collective-permute-start.11
  42.4 0.7 shard_map.67.right_ref
  43.2 0.9 shard_map.66.left_ref
  44.1 0.8 shard_map.68.middle_ref
  45.6 1.6 %shard_map.74.rest_1_ = bf16[8,2,256,128]{3,2,1,0:T(8,128)(2,1)S(1)} custom-call(s32[1]{0:T(128)} %bitcast.1.member_ref, bf16[4,2,576,128]{3,2,1,0:T(8,128)(2,1)S(1)} %shard_map.68.middle_ref, bf16[2,2,576,128]{3,2,1,0:T(8,128)(2,1)S(1)} %shard_map.69.left_ref, bf16[2,2,320,128]{3,2,1,0:T(8,128)(2,1)S(1)} %shard_map.73.right_ref, ...), custom_call_target="tpu_custom_call" | custom-call | flops 1000000000 | bytes 1048576 | tf_op jit(solution)/shard_map/pallas_call | solution.py:291
  47.2 1.6 %shard_map.71.rest_0_ = bf16[8,2,256,128]{3,2,1,0:T(8,128)(2,1)S(1)} custom-call(s32[1]{0:T(128)} %bitcast.1.member_ref, bf16[4,2,576,128]{3,2,1,0:T(8,128)(2,1)S(1)} %shard_map.68.middle_ref, bf16[2,2,576,128]{3,2,1,0:T(8,128)(2,1)S(1)} %shard_map.69.left_ref, bf16[2,2,320,128]{3,2,1,0:T(8,128)(2,1)S(1)} %shard_map.70.right_ref, ...), custom_call_target="tpu_custom_call" | custom-call | flops 1000000000 | bytes 1048576 | tf_op jit(solution)/shard_map/pallas_call | solution.py:291
  48.8 1.2 %shard_map.72.rest_0_ = bf16[8,2,16,1024]{3,2,1,0:T(8,128)(2,1)S(1)} custom-call(bf16[8,2,256,128]{3,2,1,0:T(8,128)(2,1)S(1)} %shard_map.71.rest_0_, bf16[256,512]{1,0:T(8,128)(2,1)S(1)} %bitcast.9, bf16[256,512]{1,0:T(8,128)(2,1)S(1)} %collective-permute-done.7.rest_2_.rest_3_, bf16[256,512]{1,0:T(8,128)(2,1)S(1)} %collective-permute-done.8.rest_3_.rest_4_, ...), custom_call_target="tpu_custom_call" | custom-call | flops 1000000000 | bytes 1048576 | tf_op jit(solution)/shard_map/pallas_call | solution.py:291
  50.0 1.3 %shard_map.75 = bf16[8,4,16,1024]{3,2,1,0:T(8,128)(2,1)S(1)} custom-call(bf16[8,2,16,1024]{3,2,1,0:T(8,128)(2,1)S(1)} %shard_map.72.rest_0_, bf16[8,2,256,128]{3,2,1,0:T(8,128)(2,1)S(1)} %shard_map.74.rest_1_, bf16[256,512]{1,0:T(8,128)(2,1)S(1)} %bitcast.10, bf16[256,512]{1,0:T(8,128)(2,1)S(1)} %collective-permute-done.7.rest_2_.rest_3_, ...), custom_call_target="tpu_custom_call" | custom-call | flops 1000000000 | bytes 1048576 | tf_op jit(solution)/shard_map/pallas_call | solution.py:291
  51.4 21.1 %all_to_all.10.pieces_ref = bf16[8,4,16,1024]{3,2,1,0:T(8,128)(2,1)S(1)} all-to-all(bf16[8,4,16,1024]{3,2,1,0:T(8,128)(2,1)S(1)} %shard_map.75), channel_id=1, replica_groups=mesh['pulse'=8,'tile'=32] {'pulse'}, dimensions={0} | all-to-all | bytes 2097152 | tf_op jit(solution)/shard_map/all_to_all | solution.py:408
  72.4 0.8 shard_map.76
  73.3 7.6 %all-to-all-start.1 = ((bf16[8,16,1024]{2,1,0:T(8,128)(2,1)}), bf16[8,16,1024]{2,1,0:T(8,128)(2,1)S(1)}, u32[]{:S(2)}, u32[]{:S(2)}) async-start(bf16[8,16,1024]{2,1,0:T(8,128)(2,1)} %bitcast.4), calls=%async_computation.1 | async-start | bytes 524288 | tf_op jit(solution)/shard_map/all_to_all | solution.py:426
  80.8 15.3 %all-to-all-done.1.pieces_ref = bf16[8,16,1024]{2,1,0:T(8,128)(2,1)S(1)} async-done(((bf16[8,16,1024]{2,1,0:T(8,128)(2,1)}), bf16[8,16,1024]{2,1,0:T(8,128)(2,1)S(1)}, u32[]{:S(2)}, u32[]{:S(2)}) %all-to-all-start.1) | async-done | bytes 262176 | tf_op jit(solution)/shard_map/all_to_all | solution.py:426
  96.1 0.6 shard_map.77
  (35 shorter events, 2.0 us)
Async XLA Ops:
  0.0 29.0 %copy-start.4 = (s32[3,2,128]{2,1,0:T(2,128)S(1)}, s32[3,2,128]{2,1,0:T(2,128)}, u32[]{:S(2)}) copy-start(s32[3,2,128]{2,1,0:T(2,128)} %shift_ref.5) | copy-start | bytes 9220
  0.0 1.6 %copy-start = (bf16[4096,2,128]{2,1,0:T(2,128)(2,1)S(1)}, bf16[4096,2,128]{2,1,0:T(2,128)(2,1)}, u32[]{:S(2)}) copy-start(bf16[4096,2,128]{2,1,0:T(2,128)(2,1)} %param.6) | copy-start | bytes 6291460
  1.6 3.2 %copy-start.3 = (bf16[1,1,2,128,512]{4,3,2,1,0:T(8,128)(2,1)S(1)}, bf16[1,1,2,128,512]{4,3,2,1,0:T(8,128)(2,1)}, u32[]{:S(2)}) copy-start(bf16[1,1,2,128,512]{4,3,2,1,0:T(8,128)(2,1)} %param.11) | copy-start | bytes 786436
  1.6 27.3 %copy-start.1 = (bf16[3,256,256]{2,1,0:T(8,128)(2,1)S(1)}, bf16[3,256,256]{2,1,0:T(8,128)(2,1)}, u32[]{:S(2)}) copy-start(bf16[3,256,256]{2,1,0:T(8,128)(2,1)} %merge_re_ref.1) | copy-start | bytes 1179652
  1.6 27.3 %copy-start.2 = (bf16[3,256,256]{2,1,0:T(8,128)(2,1)S(1)}, bf16[3,256,256]{2,1,0:T(8,128)(2,1)}, u32[]{:S(2)}) copy-start(bf16[3,256,256]{2,1,0:T(8,128)(2,1)} %merge_im_ref.1) | copy-start | bytes 1179652
  1.6 27.3 %copy-start.5 = (bf16[2,128,128]{2,1,0:T(8,128)(2,1)S(1)}, bf16[2,128,128]{2,1,0:T(8,128)(2,1)}, u32[]{:S(2)}) copy-start(bf16[2,128,128]{2,1,0:T(8,128)(2,1)} %steering_ref.1) | copy-start | bytes 196612
  3.1 8.9 %collective-permute-start.16 = (bf16[512,128]{1,0:T(8,128)(2,1)S(1)}, bf16[512,128]{1,0:T(8,128)(2,1)S(1)}, u32[]{:S(2)}, u32[]{:S(2)}) collective-permute-start(bf16[512,128]{1,0:T(8,128)(2,1)S(1)} %get-tuple-element.27), channel_id=1, source_target_pairs={{0,6},{1,7},{2,4},{3,5},{4,2},{5,3},{6,0},{7,1},{8,14},{9,15},{10,... | collective-permute-start | bytes 393224 | tf_op jit(solution)/shard_map/ppermute | solution.py:324
  4.8 20.8 %collective-permute-start.10 = (bf16[256,512]{1,0:T(8,128)(2,1)S(1)}, bf16[256,512]{1,0:T(8,128)(2,1)S(1)}, u32[]{:S(2)}, u32[]{:S(2)}) collective-permute-start(bf16[256,512]{1,0:T(8,128)(2,1)S(1)} %bitcast.6), channel_id=1, source_target_pairs={{0,4},{1,5},{2,6},{3,7},{4,0},{5,1},{6,2},{7,3},{8,12},{9,13},{10,... | collective-permute-start | bytes 786440 | tf_op jit(solution)/shard_map/ppermute | solution.py:324
  5.0 23.6 %collective-permute-start.8 = (bf16[256,512]{1,0:T(8,128)(2,1)S(1)}, bf16[256,512]{1,0:T(8,128)(2,1)S(1)}, u32[]{:S(2)}, u32[]{:S(2)}) collective-permute-start(bf16[256,512]{1,0:T(8,128)(2,1)S(1)} %bitcast.7), channel_id=1, source_target_pairs={{0,2},{1,3},{2,0},{3,1},{4,6},{5,7},{6,4},{7,5},{8,10},{9,11},{10,... | collective-permute-start | bytes 786440 | tf_op jit(solution)/shard_map/ppermute | solution.py:324
  8.2 13.4 %collective-permute-start.5 = (bf16[608,128]{1,0:T(8,128)(2,1)S(1)}, bf16[608,128]{1,0:T(8,128)(2,1)S(1)}, u32[]{:S(2)}, u32[]{:S(2)}) collective-permute-start(bf16[608,128]{1,0:T(8,128)(2,1)S(1)} %get-tuple-element.25), channel_id=1, source_target_pairs={{0,6},{1,7},{2,4},{3,5},{4,2},{5,3},{6,0},{7,1},{8,14},{9,15},{10,... | collective-permute-start | bytes 466952 | tf_op jit(solution)/shard_map/ppermute | solution.py:324
  9.8 11.7 %collective-permute-start.17 = (bf16[512,128]{1,0:T(8,128)(2,1)S(1)}, bf16[512,128]{1,0:T(8,128)(2,1)S(1)}, u32[]{:S(2)}, u32[]{:S(2)}) collective-permute-start(bf16[512,128]{1,0:T(8,128)(2,1)S(1)} %get-tuple-element.28), channel_id=1, source_target_pairs={{0,7},{1,6},{2,5},{3,4},{4,3},{5,2},{6,1},{7,0},{8,15},{9,14},{10,... | collective-permute-start | bytes 393224 | tf_op jit(solution)/shard_map/ppermute | solution.py:324
  12.0 13.2 %collective-permute-start.6 = (bf16[608,128]{1,0:T(8,128)(2,1)S(1)}, bf16[608,128]{1,0:T(8,128)(2,1)S(1)}, u32[]{:S(2)}, u32[]{:S(2)}) collective-permute-start(bf16[608,128]{1,0:T(8,128)(2,1)S(1)} %get-tuple-element.26), channel_id=1, source_target_pairs={{0,7},{1,6},{2,5},{3,4},{4,3},{5,2},{6,1},{7,0},{8,15},{9,14},{10,... | collective-permute-start | bytes 466952 | tf_op jit(solution)/shard_map/ppermute | solution.py:324
  21.5 8.6 %collective-permute-start.3 = (bf16[1120,128]{1,0:T(8,128)(2,1)S(1)}, bf16[1120,128]{1,0:T(8,128)(2,1)S(1)}, u32[]{:S(2)}, u32[]{:S(2)}) collective-permute-start(bf16[1120,128]{1,0:T(8,128)(2,1)S(1)} %get-tuple-element.23), channel_id=1, source_target_pairs={{0,4},{1,5},{2,6},{3,7},{4,0},{5,1},{6,2},{7,3},{8,12},{9,13},{10,... | collective-permute-start | bytes 860168 | tf_op jit(solution)/shard_map/ppermute | solution.py:324
  21.6 15.7 %collective-permute-start.4 = (bf16[1120,128]{1,0:T(8,128)(2,1)S(1)}, bf16[1120,128]{1,0:T(8,128)(2,1)S(1)}, u32[]{:S(2)}, u32[]{:S(2)}) collective-permute-start(bf16[1120,128]{1,0:T(8,128)(2,1)S(1)} %get-tuple-element.24), channel_id=1, source_target_pairs={{0,5},{1,4},{2,7},{3,6},{4,1},{5,0},{6,3},{7,2},{8,13},{9,12},{10,... | collective-permute-start | bytes 860168 | tf_op jit(solution)/shard_map/ppermute | solution.py:324
  25.2 14.3 %collective-permute-start.1 = (bf16[1120,128]{1,0:T(8,128)(2,1)S(1)}, bf16[1120,128]{1,0:T(8,128)(2,1)S(1)}, u32[]{:S(2)}, u32[]{:S(2)}) collective-permute-start(bf16[1120,128]{1,0:T(8,128)(2,1)S(1)} %get-tuple-element.21), channel_id=1, source_target_pairs={{0,2},{1,3},{2,0},{3,1},{4,6},{5,7},{6,4},{7,5},{8,10},{9,11},{10,... | collective-permute-start | bytes 860168 | tf_op jit(solution)/shard_map/ppermute | solution.py:324
  25.6 16.1 %collective-permute-start.2 = (bf16[1120,128]{1,0:T(8,128)(2,1)S(1)}, bf16[1120,128]{1,0:T(8,128)(2,1)S(1)}, u32[]{:S(2)}, u32[]{:S(2)}) collective-permute-start(bf16[1120,128]{1,0:T(8,128)(2,1)S(1)} %get-tuple-element.22), channel_id=1, source_target_pairs={{0,3},{1,2},{2,1},{3,0},{4,7},{5,6},{6,5},{7,4},{8,11},{9,10},{10,... | collective-permute-start | bytes 860168 | tf_op jit(solution)/shard_map/ppermute | solution.py:324
  28.7 14.5 %collective-permute-start = (bf16[1120,128]{1,0:T(8,128)(2,1)S(1)}, bf16[1120,128]{1,0:T(8,128)(2,1)S(1)}, u32[]{:S(2)}, u32[]{:S(2)}) collective-permute-start(bf16[1120,128]{1,0:T(8,128)(2,1)S(1)} %get-tuple-element.18), channel_id=1, source_target_pairs={{0,1},{1,0},{2,3},{3,2},{4,5},{5,4},{6,7},{7,6},{8,9},{9,8},{10,11... | collective-permute-start | bytes 860168 | tf_op jit(solution)/shard_map/ppermute | solution.py:324
  30.1 18.6 %collective-permute-start.7 = (bf16[256,512]{1,0:T(8,128)(2,1)S(1)}, bf16[256,512]{1,0:T(8,128)(2,1)S(1)}, u32[]{:S(2)}, u32[]{:S(2)}) collective-permute-start(bf16[256,512]{1,0:T(8,128)(2,1)S(1)} %bitcast.8), channel_id=1, source_target_pairs={{0,1},{1,0},{2,3},{3,2},{4,5},{5,4},{6,7},{7,6},{8,9},{9,8},{10,11... | collective-permute-start | bytes 786440 | tf_op jit(solution)/shard_map/ppermute | solution.py:324
  37.3 7.6 %collective-permute-start.12 = (bf16[128,512]{1,0:T(8,128)(2,1)S(1)}, bf16[128,512]{1,0:T(8,128)(2,1)S(1)}, u32[]{:S(2)}, u32[]{:S(2)}) collective-permute-start(bf16[128,512]{1,0:T(8,128)(2,1)S(1)} %slice.8), channel_id=1, source_target_pairs={{0,2},{1,3},{2,0},{3,1},{4,6},{5,7},{6,4},{7,5},{8,10},{9,11},{10,... | collective-permute-start | bytes 393224 | tf_op jit(solution)/shard_map/ppermute | solution.py:324
  39.5 5.9 %collective-permute-start.13 = (bf16[128,512]{1,0:T(8,128)(2,1)S(1)}, bf16[128,512]{1,0:T(8,128)(2,1)S(1)}, u32[]{:S(2)}, u32[]{:S(2)}) collective-permute-start(bf16[128,512]{1,0:T(8,128)(2,1)S(1)} %slice.9), channel_id=1, source_target_pairs={{0,4},{1,5},{2,6},{3,7},{4,0},{5,1},{6,2},{7,3},{8,12},{9,13},{10,... | collective-permute-start | bytes 393224 | tf_op jit(solution)/shard_map/ppermute | solution.py:324
  41.8 7.0 %collective-permute-start.11 = (bf16[256,512]{1,0:T(8,128)(2,1)S(1)}, bf16[256,512]{1,0:T(8,128)(2,1)S(1)}, u32[]{:S(2)}, u32[]{:S(2)}) collective-permute-start(bf16[256,512]{1,0:T(8,128)(2,1)S(1)} %collective-permute-done.10.rest_5_.rest_6_), channel_id=1, source_target_pairs={{0,1},{1,0},{2,3},{3,2},{4,5},{5,4},{6,7},{7,6},{8,9},{9,8},{10,11... | collective-permute-start | bytes 786440 | tf_op jit(solution)/shard_map/ppermute | solution.py:324
  43.1 5.7 %collective-permute-start.9 = (bf16[256,512]{1,0:T(8,128)(2,1)S(1)}, bf16[256,512]{1,0:T(8,128)(2,1)S(1)}, u32[]{:S(2)}, u32[]{:S(2)}) collective-permute-start(bf16[256,512]{1,0:T(8,128)(2,1)S(1)} %collective-permute-done.8.rest_3_.rest_4_), channel_id=1, source_target_pairs={{0,1},{1,0},{2,3},{3,2},{4,5},{5,4},{6,7},{7,6},{8,9},{9,8},{10,11... | collective-permute-start | bytes 786440 | tf_op jit(solution)/shard_map/ppermute | solution.py:324
  45.0 3.8 %collective-permute-start.14 = (bf16[128,512]{1,0:T(8,128)(2,1)S(1)}, bf16[128,512]{1,0:T(8,128)(2,1)S(1)}, u32[]{:S(2)}, u32[]{:S(2)}) collective-permute-start(bf16[128,512]{1,0:T(8,128)(2,1)S(1)} %collective-permute-done.12.rest_7_.rest_8_), channel_id=1, source_target_pairs={{0,1},{1,0},{2,3},{3,2},{4,5},{5,4},{6,7},{7,6},{8,9},{9,8},{10,11... | collective-permute-start | bytes 393224 | tf_op jit(solution)/shard_map/ppermute | solution.py:324
  45.5 3.3 %collective-permute-start.15 = (bf16[128,512]{1,0:T(8,128)(2,1)S(1)}, bf16[128,512]{1,0:T(8,128)(2,1)S(1)}, u32[]{:S(2)}, u32[]{:S(2)}) collective-permute-start(bf16[128,512]{1,0:T(8,128)(2,1)S(1)} %collective-permute-done.13.rest_8_.rest_9_), channel_id=1, source_target_pairs={{0,1},{1,0},{2,3},{3,2},{4,5},{5,4},{6,7},{7,6},{8,9},{9,8},{10,11... | collective-permute-start | bytes 393224 | tf_op jit(solution)/shard_map/ppermute | solution.py:324
  73.3 22.9 %all-to-all-start.1 = ((bf16[8,16,1024]{2,1,0:T(8,128)(2,1)}), bf16[8,16,1024]{2,1,0:T(8,128)(2,1)S(1)}, u32[]{:S(2)}, u32[]{:S(2)}) async-start(bf16[8,16,1024]{2,1,0:T(8,128)(2,1)} %bitcast.4), calls=%async_computation.1 | async-start | bytes 524288 | tf_op jit(solution)/shard_map/all_to_all | solution.py:426
where the time goes:
time: 97 us; the launch traced here: 96.8 us
  starting transfers between devices  31.2 us (32%)
  waiting for transfers between devices  29.8 us (31%)
  blocking collectives  21.1 us (22%)
  Pallas kernels  12.9 us (13%)
  local copies, waits for them, and re-layouts  1.64 us (2%)
    ppermute x18, starting transfers between devices, swap(): return lax.ppermute(value, 'tile', [(s, s ^ mask) for s in range(tiles)])  23.6 us
    all_to_all x1, blocking collectives, body(): pieces = lax.all_to_all(partial_rows, 'pulse', 0, 0, tiled=True)  21.1 us
    all_to_all x1, waiting for transfers between devices, body(): lax.all_to_all(doubled.reshape(2 * sets, piece, 2 * width), ('pulse', 'ti...  15.3 us
    ppermute x18, waiting for transfers between devices, swap(): return lax.ppermute(value, 'tile', [(s, s ^ mask) for s in range(tiles)])  14.5 us
    pallas_call x14, Pallas kernels, run(): called(kernel, out_shape, in_specs, scratch, flops, vmem, out_specs)  12.9 us
    all_to_all x1, starting transfers between devices, body(): lax.all_to_all(doubled.reshape(2 * sets, piece, 2 * width), ('pulse', 'ti...  7.56 us
  transfers between devices with their start and end apart: 19, of which 6 were waited for; matrix products, arithmetic and copies ran while one was open for 0% of the time, Pallas kernels for 8%

commit v1 on v0

--- a/solution.py
+++ b/solution.py
@@ -34,7 +34,7 @@
 
     block(steer_ref, steering_ref[0], steering_ref[1])
     for level in range(merge_re_ref.shape[0]):
-        bit = (member_ref[0] >> level) & 1
+        bit = ((member_ref[0] & (SET - 1)) >> level) & 1
         block(
             merge_ref.at[level], arranged(merge_re_ref[level], bit), arranged(merge_im_ref[level], bit)
         )
@@ -42,7 +42,7 @@
 
 def windows_kernel(own, halo, member_ref, raw_ref, *rest):
     outs, sems = rest[: SET + 2], rest[SET + 2]
-    member = member_ref[0]
+    member = (member_ref[0] & (SET - 1))
     main, edge = 2 * own, 2 * halo
     early = own + edge
 
@@ -169,7 +169,7 @@
     sources_of, rest = (rest[:many], rest[many : 2 * many]), rest[2 * many :]
     steer_ref, merge_ref, shift_ref, out_ref, beams, *sources, spread = rest
     count = steer_ref.shape[1] // 2
-    member = member_ref[0]
+    member = (member_ref[0] & (SET - 1))
     fill_guards(beams, 2, rows)
     fill_guards(out_ref, 2, rows)
     for slot, raw_refs in enumerate(sources_of):
@@ -195,7 +195,7 @@
 
 
 def middle_kernel(rows, halo, member_ref, left_ref, right_ref, merge_ref, shift_ref, out_ref, *sources):
-    member = member_ref[0]
+    member = (member_ref[0] & (SET - 1))
     fill_guards(out_ref, SET // 2, rows)
 
     def load(slot, part, window):
@@ -212,7 +212,7 @@
     rows, halo, begin, end, member_ref, middle_ref, left_ref, right_ref, merge_ref, shift_ref, out_ref,
     high, *sources,
 ):
-    member = member_ref[0]
+    member = (member_ref[0] & (SET - 1))
     fill_guards(high, SET // 2, rows)
 
     def within(window):
@@ -269,17 +269,19 @@
 
 
 def sum_kernel(pieces_ref, out_ref):
-    total = pieces_ref[0].astype(jnp.float32)
-    for source in range(1, pieces_ref.shape[0]):
-        total += pieces_ref[source].astype(jnp.float32)
-    total = total.astype(jnp.bfloat16)
-    out_ref[0] = total
-    out_ref[1] = total
+    many = pieces_ref.shape[1]
+    for at in range(many):
+        total = pieces_ref[0, at].astype(jnp.float32)
+        for source in range(1, pieces_ref.shape[0]):
+            total += pieces_ref[source, at].astype(jnp.float32)
+        total = total.astype(jnp.bfloat16)
+        out_ref[0, at] = total
+        out_ref[1, at] = total
 
 
 def last_kernel(half_ref, pieces_ref, out_ref):
     many = pieces_ref.shape[0] // 2
-    base = half_ref[0] * many
+    base = (half_ref[0] >> 3) * many
     total = pieces_ref[base].astype(jnp.float32)
     for source in range(1, many):
         total += pieces_ref[base + source].astype(jnp.float32)
@@ -318,7 +320,10 @@
     piece = own // tiles
     half_type = jnp.bfloat16
     member = lax.axis_index("tile") % SET
-    where = member.reshape(1).astype(jnp.int32)
+    pulse = lax.axis_index("pulse")
+    target = swapped(member)
+    half = jnp.where(pulse == target, pulse % 2, (pulse < target).astype(jnp.int32))
+    where = (member + SET * half).reshape(1).astype(jnp.int32)
 
     def swap(value, mask):
         return lax.ppermute(value, "tile", [(s, s ^ mask) for s in range(tiles)])
@@ -431,12 +436,9 @@
         axis_index_groups=crossing,
         tiled=True,
     )
-    pulse = lax.axis_index("pulse")
-    target = swapped(member)
-    half = jnp.where(pulse == target, pulse % 2, (pulse < target).astype(jnp.int32))
     return call(
         last_kernel, jax.ShapeDtypeStruct((piece, 2 * width), jnp.float32), [SMEM, VMEM]
-    )(half.reshape(1).astype(jnp.int32), last)
+    )(where, last)
 
 
 def solution(mesh):

time: 97 us -> 96.1 us (level)
  blocking collectives: 21.1 us -> 43.7 us
  waiting for transfers between devices: 29.8 us -> 14.5 us
  starting transfers between devices: 31.2 us -> 23.6 us
    all_to_all x0 -> x1, blocking collectives: none -> 22.6 us  [body(): lax.all_to_all(doubled.reshape(2 * sets, piece, 2 * width), ('pulse', 'ti...]
    all_to_all x1 -> x0, waiting for transfers between devices: 15.3 us -> none  [body(): lax.all_to_all(doubled.reshape(2 * sets, piece, 2 * width), ('pulse', 'ti...]
    all_to_all x1 -> x0, starting transfers between devices: 7.56 us -> none  [body(): lax.all_to_all(doubled.reshape(2 * sets, piece, 2 * width), ('pulse', 'ti...]
  transfers between devices with their start and end apart: 19 -> 18, of which waited for: 6 -> 5; matrix products, arithmetic and copies ran while one was open for 0% -> 0% of each run, Pallas kernels for 8% -> 8%
where the time goes in v1:
time: 96.1 us; the launch traced here: 95.9 us
  blocking collectives  43.7 us (45%)
  starting transfers between devices  23.6 us (25%)
  waiting for transfers between devices  14.5 us (15%)
  Pallas kernels  12.1 us (13%)
  local copies, waits for them, and re-layouts  1.66 us (2%)
    ppermute x18, starting transfers between devices, swap(): return lax.ppermute(value, 'tile', [(s, s ^ mask) for s in range(tiles)])  23.6 us
    all_to_all x1, blocking collectives, body(): lax.all_to_all(doubled.reshape(2 * sets, piece, 2 * width), ('pulse', 'ti...  22.6 us
    all_to_all x1, blocking collectives, body(): pieces = lax.all_to_all(partial_rows, 'pulse', 0, 0, tiled=True)  21.1 us
    ppermute x18, waiting for transfers between devices, swap(): return lax.ppermute(value, 'tile', [(s, s ^ mask) for s in range(tiles)])  14.5 us
    pallas_call x14, Pallas kernels, run(): called(kernel, out_shape, in_specs, scratch, flops, vmem, out_specs)  12.1 us
  transfers between devices with their start and end apart: 18, of which 5 were waited for; matrix products, arithmetic and copies ran while one was open for 0% of the time, Pallas kernels for 8%

profile of v1, /device:TPU:48, one launch (start us, length us, event | category | flops | bytes accessed | tf_op | source)
XLA Modules:
  0.0 95.9 jit_solution(8534380378365480158)
XLA Ops:
  0.0 1.6 %copy-done = bf16[4096,2,128]{2,1,0:T(2,128)(2,1)S(1)} copy-done((bf16[4096,2,128]{2,1,0:T(2,128)(2,1)S(1)}, bf16[4096,2,128]{2,1,0:T(2,128)(2,1)}, u32[]{:S(2)}) %copy-start) | copy-done | bytes 2097176
  1.6 1.5 %shard_map.64 = (bf16[1120,128]{1,0:T(8,128)(2,1)S(1)}, bf16[1120,128]{1,0:T(8,128)(2,1)S(1)}, bf16[1120,128]{1,0:T(8,128)(2,1)S(1)}, bf16[1120,128]{1,0:T(8,128...) custom-call(s32[1]{0:T(128)} %bitcast.member_ref.half_ref, ...), custom_call_target="tpu_custom_call" | custom-call | bytes 1048576 | tf_op jit(solution)/shard_map/pallas_call | solution.py:293
  3.1 1.7 %collective-permute-start.16 = (bf16[512,128]{1,0:T(8,128)(2,1)S(1)}, bf16[512,128]{1,0:T(8,128)(2,1)S(1)}, u32[]{:S(2)}, u32[]{:S(2)}) collective-permute-start(bf16[512,128]{1,0:T(8,128)(2,1)S(1)} %get-tuple-element.27), channel_id=1, source_target_pairs={{0,6},{1,7},{2,4},{3,5},{4,2},{5,3},{6,0},{7,1},{8,14},{9,15},{10,... | collective-permute-start | bytes 393224 | tf_op jit(solution)/shard_map/ppermute | solution.py:329
  5.0 3.2 %collective-permute-start.8 = (bf16[256,512]{1,0:T(8,128)(2,1)S(1)}, bf16[256,512]{1,0:T(8,128)(2,1)S(1)}, u32[]{:S(2)}, u32[]{:S(2)}) collective-permute-start(bf16[256,512]{1,0:T(8,128)(2,1)S(1)} %bitcast.7), channel_id=1, source_target_pairs={{0,2},{1,3},{2,0},{3,1},{4,6},{5,7},{6,4},{7,5},{8,10},{9,11},{10,... | collective-permute-start | bytes 786440 | tf_op jit(solution)/shard_map/ppermute | solution.py:329
  8.2 1.6 %collective-permute-start.5 = (bf16[608,128]{1,0:T(8,128)(2,1)S(1)}, bf16[608,128]{1,0:T(8,128)(2,1)S(1)}, u32[]{:S(2)}, u32[]{:S(2)}) collective-permute-start(bf16[608,128]{1,0:T(8,128)(2,1)S(1)} %get-tuple-element.25), channel_id=1, source_target_pairs={{0,6},{1,7},{2,4},{3,5},{4,2},{5,3},{6,0},{7,1},{8,14},{9,15},{10,... | collective-permute-start | bytes 466952 | tf_op jit(solution)/shard_map/ppermute | solution.py:329
  9.8 1.2 %collective-permute-start.17 = (bf16[512,128]{1,0:T(8,128)(2,1)S(1)}, bf16[512,128]{1,0:T(8,128)(2,1)S(1)}, u32[]{:S(2)}, u32[]{:S(2)}) collective-permute-start(bf16[512,128]{1,0:T(8,128)(2,1)S(1)} %get-tuple-element.28), channel_id=1, source_target_pairs={{0,7},{1,6},{2,5},{3,4},{4,3},{5,2},{6,1},{7,0},{8,15},{9,14},{10,... | collective-permute-start | bytes 393224 | tf_op jit(solution)/shard_map/ppermute | solution.py:329
  11.0 1.0 %collective-permute-done.16.rest_1_ = bf16[512,128]{1,0:T(8,128)(2,1)S(1)} collective-permute-done((bf16[512,128]{1,0:T(8,128)(2,1)S(1)}, bf16[512,128]{1,0:T(8,128)(2,1)S(1)}, u32[]{:S(2)}, u32[]{:S(2)}) %collective-permute-start.16) | collective-permute-done | bytes 131104 | tf_op jit(solution)/shard_map/ppermute | solution.py:329
  12.0 2.0 %collective-permute-start.6 = (bf16[608,128]{1,0:T(8,128)(2,1)S(1)}, bf16[608,128]{1,0:T(8,128)(2,1)S(1)}, u32[]{:S(2)}, u32[]{:S(2)}) collective-permute-start(bf16[608,128]{1,0:T(8,128)(2,1)S(1)} %get-tuple-element.26), channel_id=1, source_target_pairs={{0,7},{1,6},{2,5},{3,4},{4,3},{5,2},{6,1},{7,0},{8,15},{9,14},{10,... | collective-permute-start | bytes 466952 | tf_op jit(solution)/shard_map/ppermute | solution.py:329
  14.0 7.5 %collective-permute-done.17.rest_3_ = bf16[512,128]{1,0:T(8,128)(2,1)S(1)} collective-permute-done((bf16[512,128]{1,0:T(8,128)(2,1)S(1)}, bf16[512,128]{1,0:T(8,128)(2,1)S(1)}, u32[]{:S(2)}, u32[]{:S(2)}) %collective-permute-start.17) | collective-permute-done | bytes 131104 | tf_op jit(solution)/shard_map/ppermute | solution.py:329
  21.6 3.6 %collective-permute-start.4 = (bf16[1120,128]{1,0:T(8,128)(2,1)S(1)}, bf16[1120,128]{1,0:T(8,128)(2,1)S(1)}, u32[]{:S(2)}, u32[]{:S(2)}) collective-permute-start(bf16[1120,128]{1,0:T(8,128)(2,1)S(1)} %get-tuple-element.24), channel_id=1, source_target_pairs={{0,5},{1,4},{2,7},{3,6},{4,1},{5,0},{6,3},{7,2},{8,13},{9,12},{10,... | collective-permute-start | bytes 860168 | tf_op jit(solution)/shard_map/ppermute | solution.py:329
  25.2 0.4 collective-permute-start.1
  25.6 3.0 %collective-permute-start.2 = (bf16[1120,128]{1,0:T(8,128)(2,1)S(1)}, bf16[1120,128]{1,0:T(8,128)(2,1)S(1)}, u32[]{:S(2)}, u32[]{:S(2)}) collective-permute-start(bf16[1120,128]{1,0:T(8,128)(2,1)S(1)} %get-tuple-element.22), channel_id=1, source_target_pairs={{0,3},{1,2},{2,1},{3,0},{4,7},{5,6},{6,5},{7,4},{8,11},{9,10},{10,... | collective-permute-start | bytes 860168 | tf_op jit(solution)/shard_map/ppermute | solution.py:329
  29.0 0.5 shard_map.70.right_ref
  29.6 0.5 shard_map.73.right_ref
  30.1 2.6 %collective-permute-start.7 = (bf16[256,512]{1,0:T(8,128)(2,1)S(1)}, bf16[256,512]{1,0:T(8,128)(2,1)S(1)}, u32[]{:S(2)}, u32[]{:S(2)}) collective-permute-start(bf16[256,512]{1,0:T(8,128)(2,1)S(1)} %bitcast.8), channel_id=1, source_target_pairs={{0,1},{1,0},{2,3},{3,2},{4,5},{5,4},{6,7},{7,6},{8,9},{9,8},{10,11... | collective-permute-start | bytes 786440 | tf_op jit(solution)/shard_map/ppermute | solution.py:329
  32.7 4.6 %collective-permute-done.4.rest_1_ = bf16[1120,128]{1,0:T(8,128)(2,1)S(1)} collective-permute-done((bf16[1120,128]{1,0:T(8,128)(2,1)S(1)}, bf16[1120,128]{1,0:T(8,128)(2,1)S(1)}, u32[]{:S(2)}, u32[]{:S(2)}) %collective-permute-start.4) | collective-permute-done | bytes 286752 | tf_op jit(solution)/shard_map/ppermute | solution.py:329
  37.3 1.5 %collective-permute-start.12 = (bf16[128,512]{1,0:T(8,128)(2,1)S(1)}, bf16[128,512]{1,0:T(8,128)(2,1)S(1)}, u32[]{:S(2)}, u32[]{:S(2)}) collective-permute-start(bf16[128,512]{1,0:T(8,128)(2,1)S(1)} %slice.8), channel_id=1, source_target_pairs={{0,2},{1,3},{2,0},{3,1},{4,6},{5,7},{6,4},{7,5},{8,10},{9,11},{10,... | collective-permute-start | bytes 393224 | tf_op jit(solution)/shard_map/ppermute | solution.py:329
  38.8 0.7 shard_map.69.left_ref
  39.5 1.0 %collective-permute-start.13 = (bf16[128,512]{1,0:T(8,128)(2,1)S(1)}, bf16[128,512]{1,0:T(8,128)(2,1)S(1)}, u32[]{:S(2)}, u32[]{:S(2)}) collective-permute-start(bf16[128,512]{1,0:T(8,128)(2,1)S(1)} %slice.9), channel_id=1, source_target_pairs={{0,4},{1,5},{2,6},{3,7},{4,0},{5,1},{6,2},{7,3},{8,12},{9,13},{10,... | collective-permute-start | bytes 393224 | tf_op jit(solution)/shard_map/ppermute | solution.py:329
  40.5 1.2 %collective-permute-done.2.rest_1_ = bf16[1120,128]{1,0:T(8,128)(2,1)S(1)} collective-permute-done((bf16[1120,128]{1,0:T(8,128)(2,1)S(1)}, bf16[1120,128]{1,0:T(8,128)(2,1)S(1)}, u32[]{:S(2)}, u32[]{:S(2)}) %collective-permute-start.2) | collective-permute-done | bytes 286752 | tf_op jit(solution)/shard_map/ppermute | solution.py:329
  41.7 0.7 collective-permute-start.11
  42.4 0.7 shard_map.67.right_ref
  43.2 0.9 shard_map.66.left_ref
  44.1 0.8 shard_map.68.middle_ref
  45.0 0.5 collective-permute-start.14
  45.6 1.6 %shard_map.74.rest_1_ = bf16[8,2,256,128]{3,2,1,0:T(8,128)(2,1)S(1)} custom-call(s32[1]{0:T(128)} %bitcast.member_ref.half_ref, bf16[4,2,576,128]{3,2,1,0:T(8,128)(2,1)S(1)} %shard_map.68.middle_ref, bf16[2,2,576,128]{3,2,1,0:T(8,128)(2,1)S(1)} %shard_map.69.left_ref, bf16[2,2,320,128]{3,2,1,0:T(8,128)(2,1)S(1)} %shard_map.73.right_ref, ...), custom_call_target="tpu_custom_call" | custom-call | flops 1000000000 | bytes 1048576 | tf_op jit(solution)/shard_map/pallas_call | solution.py:293
  47.2 1.6 %shard_map.71.rest_0_ = bf16[8,2,256,128]{3,2,1,0:T(8,128)(2,1)S(1)} custom-call(s32[1]{0:T(128)} %bitcast.member_ref.half_ref, bf16[4,2,576,128]{3,2,1,0:T(8,128)(2,1)S(1)} %shard_map.68.middle_ref, bf16[2,2,576,128]{3,2,1,0:T(8,128)(2,1)S(1)} %shard_map.69.left_ref, bf16[2,2,320,128]{3,2,1,0:T(8,128)(2,1)S(1)} %shard_map.70.right_ref, ...), custom_call_target="tpu_custom_call" | custom-call | flops 1000000000 | bytes 1048576 | tf_op jit(solution)/shard_map/pallas_call | solution.py:293
  48.8 1.2 %shard_map.72.rest_0_ = bf16[8,2,16,1024]{3,2,1,0:T(8,128)(2,1)S(1)} custom-call(bf16[8,2,256,128]{3,2,1,0:T(8,128)(2,1)S(1)} %shard_map.71.rest_0_, bf16[256,512]{1,0:T(8,128)(2,1)S(1)} %bitcast.9, bf16[256,512]{1,0:T(8,128)(2,1)S(1)} %collective-permute-done.7.rest_2_.rest_3_, bf16[256,512]{1,0:T(8,128)(2,1)S(1)} %collective-permute-done.8.rest_3_.rest_4_, ...), custom_call_target="tpu_custom_call" | custom-call | flops 1000000000 | bytes 1048576 | tf_op jit(solution)/shard_map/pallas_call | solution.py:293
  50.0 1.3 %shard_map.75 = bf16[8,4,16,1024]{3,2,1,0:T(8,128)(2,1)S(1)} custom-call(bf16[8,2,16,1024]{3,2,1,0:T(8,128)(2,1)S(1)} %shard_map.72.rest_0_, bf16[8,2,256,128]{3,2,1,0:T(8,128)(2,1)S(1)} %shard_map.74.rest_1_, bf16[256,512]{1,0:T(8,128)(2,1)S(1)} %bitcast.10, bf16[256,512]{1,0:T(8,128)(2,1)S(1)} %collective-permute-done.7.rest_2_.rest_3_, ...), custom_call_target="tpu_custom_call" | custom-call | flops 1000000000 | bytes 1048576 | tf_op jit(solution)/shard_map/pallas_call | solution.py:293
  51.3 21.1 %all_to_all.10.pieces_ref = bf16[8,4,16,1024]{3,2,1,0:T(8,128)(2,1)S(1)} all-to-all(bf16[8,4,16,1024]{3,2,1,0:T(8,128)(2,1)S(1)} %shard_map.75), channel_id=1, replica_groups=mesh['pulse'=8,'tile'=32] {'pulse'}, dimensions={0} | all-to-all | bytes 2097152 | tf_op jit(solution)/shard_map/all_to_all | solution.py:413
  72.6 22.6 %all_to_all.11.pieces_ref = bf16[8,16,1024]{2,1,0:T(8,128)(2,1)S(1)} all-to-all(bf16[8,16,1024]{2,1,0:T(8,128)(2,1)S(1)} %bitcast.5), channel_id=1, replica_groups={{1,9,17,25,32,40,48,56},{4,12,20,28,64,72,80,88},{5,13,21,29,96,104,112..., dimensions={0} | all-to-all | bytes 524288 | tf_op jit(solution)/shard_map/all_to_all | solution.py:431
  95.2 0.6 shard_map.77
  (34 shorter events, 1.2 us)
Async XLA Ops:
  0.0 28.9 %copy-start.5 = (bf16[2,128,128]{2,1,0:T(8,128)(2,1)S(1)}, bf16[2,128,128]{2,1,0:T(8,128)(2,1)}, u32[]{:S(2)}) copy-start(bf16[2,128,128]{2,1,0:T(8,128)(2,1)} %steering_ref.1) | copy-start | bytes 196612
  0.0 29.0 %copy-start.4 = (s32[3,2,128]{2,1,0:T(2,128)S(1)}, s32[3,2,128]{2,1,0:T(2,128)}, u32[]{:S(2)}) copy-start(s32[3,2,128]{2,1,0:T(2,128)} %shift_ref.5) | copy-start | bytes 9220
  0.0 1.6 %copy-start = (bf16[4096,2,128]{2,1,0:T(2,128)(2,1)S(1)}, bf16[4096,2,128]{2,1,0:T(2,128)(2,1)}, u32[]{:S(2)}) copy-start(bf16[4096,2,128]{2,1,0:T(2,128)(2,1)} %param.6) | copy-start | bytes 6291460
  1.6 3.2 %copy-start.3 = (bf16[1,1,2,128,512]{4,3,2,1,0:T(8,128)(2,1)S(1)}, bf16[1,1,2,128,512]{4,3,2,1,0:T(8,128)(2,1)}, u32[]{:S(2)}) copy-start(bf16[1,1,2,128,512]{4,3,2,1,0:T(8,128)(2,1)} %param.11) | copy-start | bytes 786436
  1.6 27.3 %copy-start.1 = (bf16[3,256,256]{2,1,0:T(8,128)(2,1)S(1)}, bf16[3,256,256]{2,1,0:T(8,128)(2,1)}, u32[]{:S(2)}) copy-start(bf16[3,256,256]{2,1,0:T(8,128)(2,1)} %merge_re_ref.1) | copy-start | bytes 1179652
  1.6 27.3 %copy-start.2 = (bf16[3,256,256]{2,1,0:T(8,128)(2,1)S(1)}, bf16[3,256,256]{2,1,0:T(8,128)(2,1)}, u32[]{:S(2)}) copy-start(bf16[3,256,256]{2,1,0:T(8,128)(2,1)} %merge_im_ref.1) | copy-start | bytes 1179652
  3.1 8.9 %collective-permute-start.16 = (bf16[512,128]{1,0:T(8,128)(2,1)S(1)}, bf16[512,128]{1,0:T(8,128)(2,1)S(1)}, u32[]{:S(2)}, u32[]{:S(2)}) collective-permute-start(bf16[512,128]{1,0:T(8,128)(2,1)S(1)} %get-tuple-element.27), channel_id=1, source_target_pairs={{0,6},{1,7},{2,4},{3,5},{4,2},{5,3},{6,0},{7,1},{8,14},{9,15},{10,... | collective-permute-start | bytes 393224 | tf_op jit(solution)/shard_map/ppermute | solution.py:329
  4.8 20.8 %collective-permute-start.10 = (bf16[256,512]{1,0:T(8,128)(2,1)S(1)}, bf16[256,512]{1,0:T(8,128)(2,1)S(1)}, u32[]{:S(2)}, u32[]{:S(2)}) collective-permute-start(bf16[256,512]{1,0:T(8,128)(2,1)S(1)} %bitcast.6), channel_id=1, source_target_pairs={{0,4},{1,5},{2,6},{3,7},{4,0},{5,1},{6,2},{7,3},{8,12},{9,13},{10,... | collective-permute-start | bytes 786440 | tf_op jit(solution)/shard_map/ppermute | solution.py:329
  5.0 23.6 %collective-permute-start.8 = (bf16[256,512]{1,0:T(8,128)(2,1)S(1)}, bf16[256,512]{1,0:T(8,128)(2,1)S(1)}, u32[]{:S(2)}, u32[]{:S(2)}) collective-permute-start(bf16[256,512]{1,0:T(8,128)(2,1)S(1)} %bitcast.7), channel_id=1, source_target_pairs={{0,2},{1,3},{2,0},{3,1},{4,6},{5,7},{6,4},{7,5},{8,10},{9,11},{10,... | collective-permute-start | bytes 786440 | tf_op jit(solution)/shard_map/ppermute | solution.py:329
  8.2 13.4 %collective-permute-start.5 = (bf16[608,128]{1,0:T(8,128)(2,1)S(1)}, bf16[608,128]{1,0:T(8,128)(2,1)S(1)}, u32[]{:S(2)}, u32[]{:S(2)}) collective-permute-start(bf16[608,128]{1,0:T(8,128)(2,1)S(1)} %get-tuple-element.25), channel_id=1, source_target_pairs={{0,6},{1,7},{2,4},{3,5},{4,2},{5,3},{6,0},{7,1},{8,14},{9,15},{10,... | collective-permute-start | bytes 466952 | tf_op jit(solution)/shard_map/ppermute | solution.py:329
  9.8 11.7 %collective-permute-start.17 = (bf16[512,128]{1,0:T(8,128)(2,1)S(1)}, bf16[512,128]{1,0:T(8,128)(2,1)S(1)}, u32[]{:S(2)}, u32[]{:S(2)}) collective-permute-start(bf16[512,128]{1,0:T(8,128)(2,1)S(1)} %get-tuple-element.28), channel_id=1, source_target_pairs={{0,7},{1,6},{2,5},{3,4},{4,3},{5,2},{6,1},{7,0},{8,15},{9,14},{10,... | collective-permute-start | bytes 393224 | tf_op jit(solution)/shard_map/ppermute | solution.py:329
  12.0 13.2 %collective-permute-start.6 = (bf16[608,128]{1,0:T(8,128)(2,1)S(1)}, bf16[608,128]{1,0:T(8,128)(2,1)S(1)}, u32[]{:S(2)}, u32[]{:S(2)}) collective-permute-start(bf16[608,128]{1,0:T(8,128)(2,1)S(1)} %get-tuple-element.26), channel_id=1, source_target_pairs={{0,7},{1,6},{2,5},{3,4},{4,3},{5,2},{6,1},{7,0},{8,15},{9,14},{10,... | collective-permute-start | bytes 466952 | tf_op jit(solution)/shard_map/ppermute | solution.py:329
  21.5 8.6 %collective-permute-start.3 = (bf16[1120,128]{1,0:T(8,128)(2,1)S(1)}, bf16[1120,128]{1,0:T(8,128)(2,1)S(1)}, u32[]{:S(2)}, u32[]{:S(2)}) collective-permute-start(bf16[1120,128]{1,0:T(8,128)(2,1)S(1)} %get-tuple-element.23), channel_id=1, source_target_pairs={{0,4},{1,5},{2,6},{3,7},{4,0},{5,1},{6,2},{7,3},{8,12},{9,13},{10,... | collective-permute-start | bytes 860168 | tf_op jit(solution)/shard_map/ppermute | solution.py:329
  21.6 15.7 %collective-permute-start.4 = (bf16[1120,128]{1,0:T(8,128)(2,1)S(1)}, bf16[1120,128]{1,0:T(8,128)(2,1)S(1)}, u32[]{:S(2)}, u32[]{:S(2)}) collective-permute-start(bf16[1120,128]{1,0:T(8,128)(2,1)S(1)} %get-tuple-element.24), channel_id=1, source_target_pairs={{0,5},{1,4},{2,7},{3,6},{4,1},{5,0},{6,3},{7,2},{8,13},{9,12},{10,... | collective-permute-start | bytes 860168 | tf_op jit(solution)/shard_map/ppermute | solution.py:329
  25.2 14.3 %collective-permute-start.1 = (bf16[1120,128]{1,0:T(8,128)(2,1)S(1)}, bf16[1120,128]{1,0:T(8,128)(2,1)S(1)}, u32[]{:S(2)}, u32[]{:S(2)}) collective-permute-start(bf16[1120,128]{1,0:T(8,128)(2,1)S(1)} %get-tuple-element.21), channel_id=1, source_target_pairs={{0,2},{1,3},{2,0},{3,1},{4,6},{5,7},{6,4},{7,5},{8,10},{9,11},{10,... | collective-permute-start | bytes 860168 | tf_op jit(solution)/shard_map/ppermute | solution.py:329
  25.6 16.1 %collective-permute-start.2 = (bf16[1120,128]{1,0:T(8,128)(2,1)S(1)}, bf16[1120,128]{1,0:T(8,128)(2,1)S(1)}, u32[]{:S(2)}, u32[]{:S(2)}) collective-permute-start(bf16[1120,128]{1,0:T(8,128)(2,1)S(1)} %get-tuple-element.22), channel_id=1, source_target_pairs={{0,3},{1,2},{2,1},{3,0},{4,7},{5,6},{6,5},{7,4},{8,11},{9,10},{10,... | collective-permute-start | bytes 860168 | tf_op jit(solution)/shard_map/ppermute | solution.py:329
  28.7 14.5 %collective-permute-start = (bf16[1120,128]{1,0:T(8,128)(2,1)S(1)}, bf16[1120,128]{1,0:T(8,128)(2,1)S(1)}, u32[]{:S(2)}, u32[]{:S(2)}) collective-permute-start(bf16[1120,128]{1,0:T(8,128)(2,1)S(1)} %get-tuple-element.18), channel_id=1, source_target_pairs={{0,1},{1,0},{2,3},{3,2},{4,5},{5,4},{6,7},{7,6},{8,9},{9,8},{10,11... | collective-permute-start | bytes 860168 | tf_op jit(solution)/shard_map/ppermute | solution.py:329
  30.1 18.6 %collective-permute-start.7 = (bf16[256,512]{1,0:T(8,128)(2,1)S(1)}, bf16[256,512]{1,0:T(8,128)(2,1)S(1)}, u32[]{:S(2)}, u32[]{:S(2)}) collective-permute-start(bf16[256,512]{1,0:T(8,128)(2,1)S(1)} %bitcast.8), channel_id=1, source_target_pairs={{0,1},{1,0},{2,3},{3,2},{4,5},{5,4},{6,7},{7,6},{8,9},{9,8},{10,11... | collective-permute-start | bytes 786440 | tf_op jit(solution)/shard_map/ppermute | solution.py:329
  37.3 7.6 %collective-permute-start.12 = (bf16[128,512]{1,0:T(8,128)(2,1)S(1)}, bf16[128,512]{1,0:T(8,128)(2,1)S(1)}, u32[]{:S(2)}, u32[]{:S(2)}) collective-permute-start(bf16[128,512]{1,0:T(8,128)(2,1)S(1)} %slice.8), channel_id=1, source_target_pairs={{0,2},{1,3},{2,0},{3,1},{4,6},{5,7},{6,4},{7,5},{8,10},{9,11},{10,... | collective-permute-start | bytes 393224 | tf_op jit(solution)/shard_map/ppermute | solution.py:329
  39.5 5.9 %collective-permute-start.13 = (bf16[128,512]{1,0:T(8,128)(2,1)S(1)}, bf16[128,512]{1,0:T(8,128)(2,1)S(1)}, u32[]{:S(2)}, u32[]{:S(2)}) collective-permute-start(bf16[128,512]{1,0:T(8,128)(2,1)S(1)} %slice.9), channel_id=1, source_target_pairs={{0,4},{1,5},{2,6},{3,7},{4,0},{5,1},{6,2},{7,3},{8,12},{9,13},{10,... | collective-permute-start | bytes 393224 | tf_op jit(solution)/shard_map/ppermute | solution.py:329
  41.7 7.0 %collective-permute-start.11 = (bf16[256,512]{1,0:T(8,128)(2,1)S(1)}, bf16[256,512]{1,0:T(8,128)(2,1)S(1)}, u32[]{:S(2)}, u32[]{:S(2)}) collective-permute-start(bf16[256,512]{1,0:T(8,128)(2,1)S(1)} %collective-permute-done.10.rest_5_.rest_6_), channel_id=1, source_target_pairs={{0,1},{1,0},{2,3},{3,2},{4,5},{5,4},{6,7},{7,6},{8,9},{9,8},{10,11... | collective-permute-start | bytes 786440 | tf_op jit(solution)/shard_map/ppermute | solution.py:329
  43.1 5.7 %collective-permute-start.9 = (bf16[256,512]{1,0:T(8,128)(2,1)S(1)}, bf16[256,512]{1,0:T(8,128)(2,1)S(1)}, u32[]{:S(2)}, u32[]{:S(2)}) collective-permute-start(bf16[256,512]{1,0:T(8,128)(2,1)S(1)} %collective-permute-done.8.rest_3_.rest_4_), channel_id=1, source_target_pairs={{0,1},{1,0},{2,3},{3,2},{4,5},{5,4},{6,7},{7,6},{8,9},{9,8},{10,11... | collective-permute-start | bytes 786440 | tf_op jit(solution)/shard_map/ppermute | solution.py:329
  45.0 3.8 %collective-permute-start.14 = (bf16[128,512]{1,0:T(8,128)(2,1)S(1)}, bf16[128,512]{1,0:T(8,128)(2,1)S(1)}, u32[]{:S(2)}, u32[]{:S(2)}) collective-permute-start(bf16[128,512]{1,0:T(8,128)(2,1)S(1)} %collective-permute-done.12.rest_7_.rest_8_), channel_id=1, source_target_pairs={{0,1},{1,0},{2,3},{3,2},{4,5},{5,4},{6,7},{7,6},{8,9},{9,8},{10,11... | collective-permute-start | bytes 393224 | tf_op jit(solution)/shard_map/ppermute | solution.py:329
  45.5 3.3 %collective-permute-start.15 = (bf16[128,512]{1,0:T(8,128)(2,1)S(1)}, bf16[128,512]{1,0:T(8,128)(2,1)S(1)}, u32[]{:S(2)}, u32[]{:S(2)}) collective-permute-start(bf16[128,512]{1,0:T(8,128)(2,1)S(1)} %collective-permute-done.13.rest_8_.rest_9_), channel_id=1, source_target_pairs={{0,1},{1,0},{2,3},{3,2},{4,5},{5,4},{6,7},{7,6},{8,9},{9,8},{10,11... | collective-permute-start | bytes 393224 | tf_op jit(solution)/shard_map/ppermute | solution.py:329

commit v2 on v1

--- a/solution.py
+++ b/solution.py
@@ -275,16 +275,16 @@
         for source in range(1, pieces_ref.shape[0]):
             total += pieces_ref[source, at].astype(jnp.float32)
         total = total.astype(jnp.bfloat16)
-        out_ref[0, at] = total
-        out_ref[1, at] = total
+        out_ref[at, 0] = total
+        out_ref[at, 1] = total
 
 
 def last_kernel(half_ref, pieces_ref, out_ref):
     many = pieces_ref.shape[0] // 2
-    base = (half_ref[0] >> 3) * many
-    total = pieces_ref[base].astype(jnp.float32)
+    half = half_ref[0] >> 3
+    total = pieces_ref[half].astype(jnp.float32)
     for source in range(1, many):
-        total += pieces_ref[base + source].astype(jnp.float32)
+        total += pieces_ref[2 * source + half].astype(jnp.float32)
     out_ref[...] = total
 
 
@@ -412,7 +412,7 @@
 
     pieces = lax.all_to_all(partial_rows, "pulse", 0, 0, tiled=True)
     doubled = call(
-        sum_kernel, jax.ShapeDtypeStruct((2, sets, piece, 2 * width), half_type), [VMEM]
+        sum_kernel, jax.ShapeDtypeStruct((sets, 2, piece, 2 * width), half_type), [VMEM]
     )(pieces)
 
     def device(pulse, u, i):
@@ -421,12 +421,10 @@
     crossing = []
     for a in range(groups):
         for b in range(a + 1, groups):
-            crossing.append(
-                [device(a, u, b) for u in range(sets)] + [device(b, u, a) for u in range(sets)]
-            )
+            crossing.append([device(*end) for u in range(sets) for end in ((a, u, b), (b, u, a))])
     for a in range(0, groups, 2):
         crossing.append(
-            [device(a, u, a) for u in range(sets)] + [device(a + 1, u, a + 1) for u in range(sets)]
+            [device(*end) for u in range(sets) for end in ((a, u, a), (a + 1, u, a + 1))]
         )
     last = lax.all_to_all(
         doubled.reshape(2 * sets, piece, 2 * width),

time: 96.1 us -> 95.4 us (level)
  the two profiles are of different devices: /device:TPU:48 before, /device:TPU:40 now
where the time goes in v2:
time: 95.4 us; the launch traced here: 95.2 us
  blocking collectives  43 us (45%)
  starting transfers between devices  23.4 us (25%)
  waiting for transfers between devices  14.8 us (16%)
  Pallas kernels  12.1 us (13%)
  local copies, waits for them, and re-layouts  1.66 us (2%)
    ppermute x18, starting transfers between devices, swap(): return lax.ppermute(value, 'tile', [(s, s ^ mask) for s in range(tiles)])  23.4 us
    all_to_all x1, blocking collectives, body(): lax.all_to_all(doubled.reshape(2 * sets, piece, 2 * width), ('pulse', 'ti...  22.7 us
    all_to_all x1, blocking collectives, body(): pieces = lax.all_to_all(partial_rows, 'pulse', 0, 0, tiled=True)  20.3 us
    ppermute x18, waiting for transfers between devices, swap(): return lax.ppermute(value, 'tile', [(s, s ^ mask) for s in range(tiles)])  14.8 us
    pallas_call x14, Pallas kernels, run(): called(kernel, out_shape, in_specs, scratch, flops, vmem, out_specs)  12.1 us
  transfers between devices with their start and end apart: 18, of which 5 were waited for; matrix products, arithmetic and copies ran while one was open for 0% of the time, Pallas kernels for 8%

profile of v2, /device:TPU:40, one launch (start us, length us, event | category | flops | bytes accessed | tf_op | source)
XLA Modules:
  0.0 95.2 jit_solution(13892018983537826151)
XLA Ops:
  0.0 1.6 %copy-done = bf16[4096,2,128]{2,1,0:T(2,128)(2,1)S(1)} copy-done((bf16[4096,2,128]{2,1,0:T(2,128)(2,1)S(1)}, bf16[4096,2,128]{2,1,0:T(2,128)(2,1)}, u32[]{:S(2)}) %copy-start) | copy-done | bytes 2097176
  1.6 1.5 %shard_map.64 = (bf16[1120,128]{1,0:T(8,128)(2,1)S(1)}, bf16[1120,128]{1,0:T(8,128)(2,1)S(1)}, bf16[1120,128]{1,0:T(8,128)(2,1)S(1)}, bf16[1120,128]{1,0:T(8,128...) custom-call(s32[1]{0:T(128)} %bitcast.member_ref.half_ref, ...), custom_call_target="tpu_custom_call" | custom-call | bytes 1048576 | tf_op jit(solution)/shard_map/pallas_call | solution.py:293
  3.1 1.9 %collective-permute-start.16 = (bf16[512,128]{1,0:T(8,128)(2,1)S(1)}, bf16[512,128]{1,0:T(8,128)(2,1)S(1)}, u32[]{:S(2)}, u32[]{:S(2)}) collective-permute-start(bf16[512,128]{1,0:T(8,128)(2,1)S(1)} %get-tuple-element.27), channel_id=1, source_target_pairs={{0,6},{1,7},{2,4},{3,5},{4,2},{5,3},{6,0},{7,1},{8,14},{9,15},{10,... | collective-permute-start | bytes 393224 | tf_op jit(solution)/shard_map/ppermute | solution.py:329
  5.1 1.9 %collective-permute-start.10 = (bf16[256,512]{1,0:T(8,128)(2,1)S(1)}, bf16[256,512]{1,0:T(8,128)(2,1)S(1)}, u32[]{:S(2)}, u32[]{:S(2)}) collective-permute-start(bf16[256,512]{1,0:T(8,128)(2,1)S(1)} %bitcast.6), channel_id=1, source_target_pairs={{0,4},{1,5},{2,6},{3,7},{4,0},{5,1},{6,2},{7,3},{8,12},{9,13},{10,... | collective-permute-start | bytes 786440 | tf_op jit(solution)/shard_map/ppermute | solution.py:329
  7.0 1.2 %collective-permute-start.8 = (bf16[256,512]{1,0:T(8,128)(2,1)S(1)}, bf16[256,512]{1,0:T(8,128)(2,1)S(1)}, u32[]{:S(2)}, u32[]{:S(2)}) collective-permute-start(bf16[256,512]{1,0:T(8,128)(2,1)S(1)} %bitcast.7), channel_id=1, source_target_pairs={{0,2},{1,3},{2,0},{3,1},{4,6},{5,7},{6,4},{7,5},{8,10},{9,11},{10,... | collective-permute-start | bytes 786440 | tf_op jit(solution)/shard_map/ppermute | solution.py:329
  8.2 1.8 %collective-permute-start.5 = (bf16[608,128]{1,0:T(8,128)(2,1)S(1)}, bf16[608,128]{1,0:T(8,128)(2,1)S(1)}, u32[]{:S(2)}, u32[]{:S(2)}) collective-permute-start(bf16[608,128]{1,0:T(8,128)(2,1)S(1)} %get-tuple-element.25), channel_id=1, source_target_pairs={{0,6},{1,7},{2,4},{3,5},{4,2},{5,3},{6,0},{7,1},{8,14},{9,15},{10,... | collective-permute-start | bytes 466952 | tf_op jit(solution)/shard_map/ppermute | solution.py:329
  10.1 0.9 collective-permute-start.17
  11.0 1.0 %collective-permute-done.16.rest_1_ = bf16[512,128]{1,0:T(8,128)(2,1)S(1)} collective-permute-done((bf16[512,128]{1,0:T(8,128)(2,1)S(1)}, bf16[512,128]{1,0:T(8,128)(2,1)S(1)}, u32[]{:S(2)}, u32[]{:S(2)}) %collective-permute-start.16) | collective-permute-done | bytes 131104 | tf_op jit(solution)/shard_map/ppermute | solution.py:329
  12.0 2.2 %collective-permute-start.6 = (bf16[608,128]{1,0:T(8,128)(2,1)S(1)}, bf16[608,128]{1,0:T(8,128)(2,1)S(1)}, u32[]{:S(2)}, u32[]{:S(2)}) collective-permute-start(bf16[608,128]{1,0:T(8,128)(2,1)S(1)} %get-tuple-element.26), channel_id=1, source_target_pairs={{0,7},{1,6},{2,5},{3,4},{4,3},{5,2},{6,1},{7,0},{8,15},{9,14},{10,... | collective-permute-start | bytes 466952 | tf_op jit(solution)/shard_map/ppermute | solution.py:329
  14.2 7.4 %collective-permute-done.17.rest_3_ = bf16[512,128]{1,0:T(8,128)(2,1)S(1)} collective-permute-done((bf16[512,128]{1,0:T(8,128)(2,1)S(1)}, bf16[512,128]{1,0:T(8,128)(2,1)S(1)}, u32[]{:S(2)}, u32[]{:S(2)}) %collective-permute-start.17) | collective-permute-done | bytes 131104 | tf_op jit(solution)/shard_map/ppermute | solution.py:329
  21.6 1.0 %collective-permute-start.3 = (bf16[1120,128]{1,0:T(8,128)(2,1)S(1)}, bf16[1120,128]{1,0:T(8,128)(2,1)S(1)}, u32[]{:S(2)}, u32[]{:S(2)}) collective-permute-start(bf16[1120,128]{1,0:T(8,128)(2,1)S(1)} %get-tuple-element.23), channel_id=1, source_target_pairs={{0,4},{1,5},{2,6},{3,7},{4,0},{5,1},{6,2},{7,3},{8,12},{9,13},{10,... | collective-permute-start | bytes 860168 | tf_op jit(solution)/shard_map/ppermute | solution.py:329
  22.6 2.6 %collective-permute-start.4 = (bf16[1120,128]{1,0:T(8,128)(2,1)S(1)}, bf16[1120,128]{1,0:T(8,128)(2,1)S(1)}, u32[]{:S(2)}, u32[]{:S(2)}) collective-permute-start(bf16[1120,128]{1,0:T(8,128)(2,1)S(1)} %get-tuple-element.24), channel_id=1, source_target_pairs={{0,5},{1,4},{2,7},{3,6},{4,1},{5,0},{6,3},{7,2},{8,13},{9,12},{10,... | collective-permute-start | bytes 860168 | tf_op jit(solution)/shard_map/ppermute | solution.py:329
  25.3 2.2 %collective-permute-start.1 = (bf16[1120,128]{1,0:T(8,128)(2,1)S(1)}, bf16[1120,128]{1,0:T(8,128)(2,1)S(1)}, u32[]{:S(2)}, u32[]{:S(2)}) collective-permute-start(bf16[1120,128]{1,0:T(8,128)(2,1)S(1)} %get-tuple-element.21), channel_id=1, source_target_pairs={{0,2},{1,3},{2,0},{3,1},{4,6},{5,7},{6,4},{7,5},{8,10},{9,11},{10,... | collective-permute-start | bytes 860168 | tf_op jit(solution)/shard_map/ppermute | solution.py:329
  27.5 1.2 %collective-permute-start.2 = (bf16[1120,128]{1,0:T(8,128)(2,1)S(1)}, bf16[1120,128]{1,0:T(8,128)(2,1)S(1)}, u32[]{:S(2)}, u32[]{:S(2)}) collective-permute-start(bf16[1120,128]{1,0:T(8,128)(2,1)S(1)} %get-tuple-element.22), channel_id=1, source_target_pairs={{0,3},{1,2},{2,1},{3,0},{4,7},{5,6},{6,5},{7,4},{8,11},{9,10},{10,... | collective-permute-start | bytes 860168 | tf_op jit(solution)/shard_map/ppermute | solution.py:329
  29.1 0.5 shard_map.70.right_ref
  29.6 0.5 shard_map.73.right_ref
  30.2 2.6 %collective-permute-start.7 = (bf16[256,512]{1,0:T(8,128)(2,1)S(1)}, bf16[256,512]{1,0:T(8,128)(2,1)S(1)}, u32[]{:S(2)}, u32[]{:S(2)}) collective-permute-start(bf16[256,512]{1,0:T(8,128)(2,1)S(1)} %bitcast.8), channel_id=1, source_target_pairs={{0,1},{1,0},{2,3},{3,2},{4,5},{5,4},{6,7},{7,6},{8,9},{9,8},{10,11... | collective-permute-start | bytes 786440 | tf_op jit(solution)/shard_map/ppermute | solution.py:329
  32.8 4.8 %collective-permute-done.4.rest_1_ = bf16[1120,128]{1,0:T(8,128)(2,1)S(1)} collective-permute-done((bf16[1120,128]{1,0:T(8,128)(2,1)S(1)}, bf16[1120,128]{1,0:T(8,128)(2,1)S(1)}, u32[]{:S(2)}, u32[]{:S(2)}) %collective-permute-start.4) | collective-permute-done | bytes 286752 | tf_op jit(solution)/shard_map/ppermute | solution.py:329
  37.6 2.1 %collective-permute-start.12 = (bf16[128,512]{1,0:T(8,128)(2,1)S(1)}, bf16[128,512]{1,0:T(8,128)(2,1)S(1)}, u32[]{:S(2)}, u32[]{:S(2)}) collective-permute-start(bf16[128,512]{1,0:T(8,128)(2,1)S(1)} %slice.8), channel_id=1, source_target_pairs={{0,2},{1,3},{2,0},{3,1},{4,6},{5,7},{6,4},{7,5},{8,10},{9,11},{10,... | collective-permute-start | bytes 393224 | tf_op jit(solution)/shard_map/ppermute | solution.py:329
  39.6 0.7 shard_map.69.left_ref
  40.6 1.3 %collective-permute-done.2.rest_1_ = bf16[1120,128]{1,0:T(8,128)(2,1)S(1)} collective-permute-done((bf16[1120,128]{1,0:T(8,128)(2,1)S(1)}, bf16[1120,128]{1,0:T(8,128)(2,1)S(1)}, u32[]{:S(2)}, u32[]{:S(2)}) %collective-permute-start.2) | collective-permute-done | bytes 286752 | tf_op jit(solution)/shard_map/ppermute | solution.py:329
  41.9 0.6 collective-permute-start.11
  42.5 0.7 shard_map.67.right_ref
  43.3 0.9 shard_map.66.left_ref
  44.1 0.8 shard_map.68.middle_ref
  45.6 1.6 %shard_map.74.rest_1_ = bf16[8,2,256,128]{3,2,1,0:T(8,128)(2,1)S(1)} custom-call(s32[1]{0:T(128)} %bitcast.member_ref.half_ref, bf16[4,2,576,128]{3,2,1,0:T(8,128)(2,1)S(1)} %shard_map.68.middle_ref, bf16[2,2,576,128]{3,2,1,0:T(8,128)(2,1)S(1)} %shard_map.69.left_ref, bf16[2,2,320,128]{3,2,1,0:T(8,128)(2,1)S(1)} %shard_map.73.right_ref, ...), custom_call_target="tpu_custom_call" | custom-call | flops 1000000000 | bytes 1048576 | tf_op jit(solution)/shard_map/pallas_call | solution.py:293
  47.2 1.6 %shard_map.71.rest_0_ = bf16[8,2,256,128]{3,2,1,0:T(8,128)(2,1)S(1)} custom-call(s32[1]{0:T(128)} %bitcast.member_ref.half_ref, bf16[4,2,576,128]{3,2,1,0:T(8,128)(2,1)S(1)} %shard_map.68.middle_ref, bf16[2,2,576,128]{3,2,1,0:T(8,128)(2,1)S(1)} %shard_map.69.left_ref, bf16[2,2,320,128]{3,2,1,0:T(8,128)(2,1)S(1)} %shard_map.70.right_ref, ...), custom_call_target="tpu_custom_call" | custom-call | flops 1000000000 | bytes 1048576 | tf_op jit(solution)/shard_map/pallas_call | solution.py:293
  48.8 1.2 %shard_map.72.rest_0_ = bf16[8,2,16,1024]{3,2,1,0:T(8,128)(2,1)S(1)} custom-call(bf16[8,2,256,128]{3,2,1,0:T(8,128)(2,1)S(1)} %shard_map.71.rest_0_, bf16[256,512]{1,0:T(8,128)(2,1)S(1)} %bitcast.9, bf16[256,512]{1,0:T(8,128)(2,1)S(1)} %collective-permute-done.7.rest_2_.rest_3_, bf16[256,512]{1,0:T(8,128)(2,1)S(1)} %collective-permute-done.8.rest_3_.rest_4_, ...), custom_call_target="tpu_custom_call" | custom-call | flops 1000000000 | bytes 1048576 | tf_op jit(solution)/shard_map/pallas_call | solution.py:293
  50.1 1.3 %shard_map.75 = bf16[8,4,16,1024]{3,2,1,0:T(8,128)(2,1)S(1)} custom-call(bf16[8,2,16,1024]{3,2,1,0:T(8,128)(2,1)S(1)} %shard_map.72.rest_0_, bf16[8,2,256,128]{3,2,1,0:T(8,128)(2,1)S(1)} %shard_map.74.rest_1_, bf16[256,512]{1,0:T(8,128)(2,1)S(1)} %bitcast.10, bf16[256,512]{1,0:T(8,128)(2,1)S(1)} %collective-permute-done.7.rest_2_.rest_3_, ...), custom_call_target="tpu_custom_call" | custom-call | flops 1000000000 | bytes 1048576 | tf_op jit(solution)/shard_map/pallas_call | solution.py:293
  51.4 20.3 %all_to_all.10.pieces_ref = bf16[8,4,16,1024]{3,2,1,0:T(8,128)(2,1)S(1)} all-to-all(bf16[8,4,16,1024]{3,2,1,0:T(8,128)(2,1)S(1)} %shard_map.75), channel_id=1, replica_groups=mesh['pulse'=8,'tile'=32] {'pulse'}, dimensions={0} | all-to-all | bytes 2097152 | tf_op jit(solution)/shard_map/all_to_all | solution.py:413
  71.9 22.7 %all_to_all.11.pieces_ref = bf16[8,16,1024]{2,1,0:T(8,128)(2,1)S(1)} all-to-all(bf16[8,16,1024]{2,1,0:T(8,128)(2,1)S(1)} %bitcast.5), channel_id=1, replica_groups={{1,32,9,40,17,48,25,56},{4,64,12,72,20,80,28,88},{5,96,13,104,21,112,29..., dimensions={0} | all-to-all | bytes 524288 | tf_op jit(solution)/shard_map/all_to_all | solution.py:429
  94.6 0.6 shard_map.77
  (34 shorter events, 1.6 us)
Async XLA Ops:
  0.0 28.9 %copy-start.5 = (bf16[2,128,128]{2,1,0:T(8,128)(2,1)S(1)}, bf16[2,128,128]{2,1,0:T(8,128)(2,1)}, u32[]{:S(2)}) copy-start(bf16[2,128,128]{2,1,0:T(8,128)(2,1)} %steering_ref.1) | copy-start | bytes 196612
  0.0 29.1 %copy-start.4 = (s32[3,2,128]{2,1,0:T(2,128)S(1)}, s32[3,2,128]{2,1,0:T(2,128)}, u32[]{:S(2)}) copy-start(s32[3,2,128]{2,1,0:T(2,128)} %shift_ref.5) | copy-start | bytes 9220
  0.0 1.6 %copy-start = (bf16[4096,2,128]{2,1,0:T(2,128)(2,1)S(1)}, bf16[4096,2,128]{2,1,0:T(2,128)(2,1)}, u32[]{:S(2)}) copy-start(bf16[4096,2,128]{2,1,0:T(2,128)(2,1)} %param.6) | copy-start | bytes 6291460
  1.6 3.5 %copy-start.3 = (bf16[1,1,2,128,512]{4,3,2,1,0:T(8,128)(2,1)S(1)}, bf16[1,1,2,128,512]{4,3,2,1,0:T(8,128)(2,1)}, u32[]{:S(2)}) copy-start(bf16[1,1,2,128,512]{4,3,2,1,0:T(8,128)(2,1)} %param.11) | copy-start | bytes 786436
  1.6 27.3 %copy-start.1 = (bf16[3,256,256]{2,1,0:T(8,128)(2,1)S(1)}, bf16[3,256,256]{2,1,0:T(8,128)(2,1)}, u32[]{:S(2)}) copy-start(bf16[3,256,256]{2,1,0:T(8,128)(2,1)} %merge_re_ref.1) | copy-start | bytes 1179652
  1.6 27.3 %copy-start.2 = (bf16[3,256,256]{2,1,0:T(8,128)(2,1)S(1)}, bf16[3,256,256]{2,1,0:T(8,128)(2,1)}, u32[]{:S(2)}) copy-start(bf16[3,256,256]{2,1,0:T(8,128)(2,1)} %merge_im_ref.1) | copy-start | bytes 1179652
  3.1 8.9 %collective-permute-start.16 = (bf16[512,128]{1,0:T(8,128)(2,1)S(1)}, bf16[512,128]{1,0:T(8,128)(2,1)S(1)}, u32[]{:S(2)}, u32[]{:S(2)}) collective-permute-start(bf16[512,128]{1,0:T(8,128)(2,1)S(1)} %get-tuple-element.27), channel_id=1, source_target_pairs={{0,6},{1,7},{2,4},{3,5},{4,2},{5,3},{6,0},{7,1},{8,14},{9,15},{10,... | collective-permute-start | bytes 393224 | tf_op jit(solution)/shard_map/ppermute | solution.py:329
  5.1 22.5 %collective-permute-start.10 = (bf16[256,512]{1,0:T(8,128)(2,1)S(1)}, bf16[256,512]{1,0:T(8,128)(2,1)S(1)}, u32[]{:S(2)}, u32[]{:S(2)}) collective-permute-start(bf16[256,512]{1,0:T(8,128)(2,1)S(1)} %bitcast.6), channel_id=1, source_target_pairs={{0,4},{1,5},{2,6},{3,7},{4,0},{5,1},{6,2},{7,3},{8,12},{9,13},{10,... | collective-permute-start | bytes 786440 | tf_op jit(solution)/shard_map/ppermute | solution.py:329
  7.0 21.8 %collective-permute-start.8 = (bf16[256,512]{1,0:T(8,128)(2,1)S(1)}, bf16[256,512]{1,0:T(8,128)(2,1)S(1)}, u32[]{:S(2)}, u32[]{:S(2)}) collective-permute-start(bf16[256,512]{1,0:T(8,128)(2,1)S(1)} %bitcast.7), channel_id=1, source_target_pairs={{0,2},{1,3},{2,0},{3,1},{4,6},{5,7},{6,4},{7,5},{8,10},{9,11},{10,... | collective-permute-start | bytes 786440 | tf_op jit(solution)/shard_map/ppermute | solution.py:329
  8.2 14.4 %collective-permute-start.5 = (bf16[608,128]{1,0:T(8,128)(2,1)S(1)}, bf16[608,128]{1,0:T(8,128)(2,1)S(1)}, u32[]{:S(2)}, u32[]{:S(2)}) collective-permute-start(bf16[608,128]{1,0:T(8,128)(2,1)S(1)} %get-tuple-element.25), channel_id=1, source_target_pairs={{0,6},{1,7},{2,4},{3,5},{4,2},{5,3},{6,0},{7,1},{8,14},{9,15},{10,... | collective-permute-start | bytes 466952 | tf_op jit(solution)/shard_map/ppermute | solution.py:329
  10.1 11.5 %collective-permute-start.17 = (bf16[512,128]{1,0:T(8,128)(2,1)S(1)}, bf16[512,128]{1,0:T(8,128)(2,1)S(1)}, u32[]{:S(2)}, u32[]{:S(2)}) collective-permute-start(bf16[512,128]{1,0:T(8,128)(2,1)S(1)} %get-tuple-element.28), channel_id=1, source_target_pairs={{0,7},{1,6},{2,5},{3,4},{4,3},{5,2},{6,1},{7,0},{8,15},{9,14},{10,... | collective-permute-start | bytes 393224 | tf_op jit(solution)/shard_map/ppermute | solution.py:329
  12.0 13.3 %collective-permute-start.6 = (bf16[608,128]{1,0:T(8,128)(2,1)S(1)}, bf16[608,128]{1,0:T(8,128)(2,1)S(1)}, u32[]{:S(2)}, u32[]{:S(2)}) collective-permute-start(bf16[608,128]{1,0:T(8,128)(2,1)S(1)} %get-tuple-element.26), channel_id=1, source_target_pairs={{0,7},{1,6},{2,5},{3,4},{4,3},{5,2},{6,1},{7,0},{8,15},{9,14},{10,... | collective-permute-start | bytes 466952 | tf_op jit(solution)/shard_map/ppermute | solution.py:329
  21.6 8.6 %collective-permute-start.3 = (bf16[1120,128]{1,0:T(8,128)(2,1)S(1)}, bf16[1120,128]{1,0:T(8,128)(2,1)S(1)}, u32[]{:S(2)}, u32[]{:S(2)}) collective-permute-start(bf16[1120,128]{1,0:T(8,128)(2,1)S(1)} %get-tuple-element.23), channel_id=1, source_target_pairs={{0,4},{1,5},{2,6},{3,7},{4,0},{5,1},{6,2},{7,3},{8,12},{9,13},{10,... | collective-permute-start | bytes 860168 | tf_op jit(solution)/shard_map/ppermute | solution.py:329
  22.6 14.9 %collective-permute-start.4 = (bf16[1120,128]{1,0:T(8,128)(2,1)S(1)}, bf16[1120,128]{1,0:T(8,128)(2,1)S(1)}, u32[]{:S(2)}, u32[]{:S(2)}) collective-permute-start(bf16[1120,128]{1,0:T(8,128)(2,1)S(1)} %get-tuple-element.24), channel_id=1, source_target_pairs={{0,5},{1,4},{2,7},{3,6},{4,1},{5,0},{6,3},{7,2},{8,13},{9,12},{10,... | collective-permute-start | bytes 860168 | tf_op jit(solution)/shard_map/ppermute | solution.py:329
  25.3 15.0 %collective-permute-start.1 = (bf16[1120,128]{1,0:T(8,128)(2,1)S(1)}, bf16[1120,128]{1,0:T(8,128)(2,1)S(1)}, u32[]{:S(2)}, u32[]{:S(2)}) collective-permute-start(bf16[1120,128]{1,0:T(8,128)(2,1)S(1)} %get-tuple-element.21), channel_id=1, source_target_pairs={{0,2},{1,3},{2,0},{3,1},{4,6},{5,7},{6,4},{7,5},{8,10},{9,11},{10,... | collective-permute-start | bytes 860168 | tf_op jit(solution)/shard_map/ppermute | solution.py:329
  27.5 14.4 %collective-permute-start.2 = (bf16[1120,128]{1,0:T(8,128)(2,1)S(1)}, bf16[1120,128]{1,0:T(8,128)(2,1)S(1)}, u32[]{:S(2)}, u32[]{:S(2)}) collective-permute-start(bf16[1120,128]{1,0:T(8,128)(2,1)S(1)} %get-tuple-element.22), channel_id=1, source_target_pairs={{0,3},{1,2},{2,1},{3,0},{4,7},{5,6},{6,5},{7,4},{8,11},{9,10},{10,... | collective-permute-start | bytes 860168 | tf_op jit(solution)/shard_map/ppermute | solution.py:329
  28.8 14.4 %collective-permute-start = (bf16[1120,128]{1,0:T(8,128)(2,1)S(1)}, bf16[1120,128]{1,0:T(8,128)(2,1)S(1)}, u32[]{:S(2)}, u32[]{:S(2)}) collective-permute-start(bf16[1120,128]{1,0:T(8,128)(2,1)S(1)} %get-tuple-element.18), channel_id=1, source_target_pairs={{0,1},{1,0},{2,3},{3,2},{4,5},{5,4},{6,7},{7,6},{8,9},{9,8},{10,11... | collective-permute-start | bytes 860168 | tf_op jit(solution)/shard_map/ppermute | solution.py:329
  30.2 18.6 %collective-permute-start.7 = (bf16[256,512]{1,0:T(8,128)(2,1)S(1)}, bf16[256,512]{1,0:T(8,128)(2,1)S(1)}, u32[]{:S(2)}, u32[]{:S(2)}) collective-permute-start(bf16[256,512]{1,0:T(8,128)(2,1)S(1)} %bitcast.8), channel_id=1, source_target_pairs={{0,1},{1,0},{2,3},{3,2},{4,5},{5,4},{6,7},{7,6},{8,9},{9,8},{10,11... | collective-permute-start | bytes 786440 | tf_op jit(solution)/shard_map/ppermute | solution.py:329
  37.6 7.5 %collective-permute-start.12 = (bf16[128,512]{1,0:T(8,128)(2,1)S(1)}, bf16[128,512]{1,0:T(8,128)(2,1)S(1)}, u32[]{:S(2)}, u32[]{:S(2)}) collective-permute-start(bf16[128,512]{1,0:T(8,128)(2,1)S(1)} %slice.8), channel_id=1, source_target_pairs={{0,2},{1,3},{2,0},{3,1},{4,6},{5,7},{6,4},{7,5},{8,10},{9,11},{10,... | collective-permute-start | bytes 393224 | tf_op jit(solution)/shard_map/ppermute | solution.py:329
  40.3 5.2 %collective-permute-start.13 = (bf16[128,512]{1,0:T(8,128)(2,1)S(1)}, bf16[128,512]{1,0:T(8,128)(2,1)S(1)}, u32[]{:S(2)}, u32[]{:S(2)}) collective-permute-start(bf16[128,512]{1,0:T(8,128)(2,1)S(1)} %slice.9), channel_id=1, source_target_pairs={{0,4},{1,5},{2,6},{3,7},{4,0},{5,1},{6,2},{7,3},{8,12},{9,13},{10,... | collective-permute-start | bytes 393224 | tf_op jit(solution)/shard_map/ppermute | solution.py:329
  41.9 6.9 %collective-permute-start.11 = (bf16[256,512]{1,0:T(8,128)(2,1)S(1)}, bf16[256,512]{1,0:T(8,128)(2,1)S(1)}, u32[]{:S(2)}, u32[]{:S(2)}) collective-permute-start(bf16[256,512]{1,0:T(8,128)(2,1)S(1)} %collective-permute-done.10.rest_5_.rest_6_), channel_id=1, source_target_pairs={{0,1},{1,0},{2,3},{3,2},{4,5},{5,4},{6,7},{7,6},{8,9},{9,8},{10,11... | collective-permute-start | bytes 786440 | tf_op jit(solution)/shard_map/ppermute | solution.py:329
  43.2 5.7 %collective-permute-start.9 = (bf16[256,512]{1,0:T(8,128)(2,1)S(1)}, bf16[256,512]{1,0:T(8,128)(2,1)S(1)}, u32[]{:S(2)}, u32[]{:S(2)}) collective-permute-start(bf16[256,512]{1,0:T(8,128)(2,1)S(1)} %collective-permute-done.8.rest_3_.rest_4_), channel_id=1, source_target_pairs={{0,1},{1,0},{2,3},{3,2},{4,5},{5,4},{6,7},{7,6},{8,9},{9,8},{10,11... | collective-permute-start | bytes 786440 | tf_op jit(solution)/shard_map/ppermute | solution.py:329
  45.1 3.7 %collective-permute-start.14 = (bf16[128,512]{1,0:T(8,128)(2,1)S(1)}, bf16[128,512]{1,0:T(8,128)(2,1)S(1)}, u32[]{:S(2)}, u32[]{:S(2)}) collective-permute-start(bf16[128,512]{1,0:T(8,128)(2,1)S(1)} %collective-permute-done.12.rest_7_.rest_8_), channel_id=1, source_target_pairs={{0,1},{1,0},{2,3},{3,2},{4,5},{5,4},{6,7},{7,6},{8,9},{9,8},{10,11... | collective-permute-start | bytes 393224 | tf_op jit(solution)/shard_map/ppermute | solution.py:329
  45.5 3.3 %collective-permute-start.15 = (bf16[128,512]{1,0:T(8,128)(2,1)S(1)}, bf16[128,512]{1,0:T(8,128)(2,1)S(1)}, u32[]{:S(2)}, u32[]{:S(2)}) collective-permute-start(bf16[128,512]{1,0:T(8,128)(2,1)S(1)} %collective-permute-done.13.rest_8_.rest_9_), channel_id=1, source_target_pairs={{0,1},{1,0},{2,3},{3,2},{4,5},{5,4},{6,7},{7,6},{8,9},{9,8},{10,11... | collective-permute-start | bytes 393224 | tf_op jit(solution)/shard_map/ppermute | solution.py:329
